TPU v7x, 32 devices: a whole 2x2x4 slice. The times are simulated.
32 devices in a mesh: gz: 4 (over z), gy: 2 (over y), gx: 4 (over x, core).
Axes of the slice: x: 2, y: 2, z: 4, core: 2. Of those that a mesh axis runs over, the one named last changes fastest.
Arguments:
- nz_vals: float32 [2097152], P(('gz', 'gy', 'gx'))
- idx_i: int32 [2097152], P(('gz', 'gy', 'gx'))
- idx_j: int32 [2097152], P(('gz', 'gy', 'gx'))
- idx_k: int32 [2097152], P(('gz', 'gy', 'gx'))
- fac_a: float32 [301056, 64], P(('gx', 'gz', 'gy'))
- fac_b: float32 [110592, 64], P(('gy', 'gz', 'gx'))
- fac_c: float32 [112640, 64], P(('gz', 'gy', 'gx'))
Outputs:
- output 1: float32 [301056, 64], P(('gx', 'gz', 'gy'))
- output 2: float32 [110592, 64], P(('gy', 'gz', 'gx'))
- output 3: float32 [112640, 64], P(('gz', 'gy', 'gx'))
- output 4: float32 [64], replicated
All inputs are finite; a program needn't handle non-finite values.
Results may differ from a plain program's by a relative error of at most 0.001.
Values are sent between devices in bfloat16 or wider.
A program may use at most 1 GiB of HBM per device.

v0:
```python
import jax
import jax.numpy as jnp
from jax import lax
from jax.sharding import PartitionSpec as P

FULL_PREC = lax.Precision.HIGHEST
PROX_WEIGHT = 0.5
ALL_AXES = ("gz", "gy", "gx")


def gram_all(fac):
    part_gram = jnp.einsum("nr,ns->rs", fac, fac, precision=FULL_PREC, preferred_element_type=jnp.float32)
    return lax.psum(part_gram, ALL_AXES)


def slab_product(nz_vals, out_rows, rows_one, rows_two, buf_one, buf_two, slab_rows):
    picked_one = jnp.take(buf_one, rows_one, axis=0).astype(jnp.float32)
    picked_two = jnp.take(buf_two, rows_two, axis=0).astype(jnp.float32)
    contrib = nz_vals[:, None] * (picked_one * picked_two)
    return jax.ops.segment_sum(contrib, out_rows, num_segments=slab_rows)


def spd_inverse(sys_mat):
    mat_order = sys_mat.shape[0]
    row_ids = jnp.arange(mat_order)[:, None]
    augmented = jnp.concatenate([sys_mat, jnp.eye(mat_order, dtype=sys_mat.dtype)], axis=1)

    def value_a9(pivot_idx, aug_rows):
        pivot_row = lax.dynamic_slice_in_dim(aug_rows, pivot_idx, 1, axis=0)
        pivot_val = lax.dynamic_slice_in_dim(pivot_row, pivot_idx, 1, axis=1)
        pivot_row = pivot_row / pivot_val
        pivot_col = lax.dynamic_slice_in_dim(aug_rows, pivot_idx, 1, axis=1)
        return jnp.where(row_ids == pivot_idx, pivot_row, aug_rows - pivot_col * pivot_row)

    augmented = lax.fori_loop(0, mat_order, value_a9, augmented)
    return augmented[:, mat_order:]


def update_owned(m_own, old_own, gram_one, gram_two, total_rows):
    gram_mat = gram_one * gram_two
    rank_size = gram_mat.shape[0]
    prox_term = PROX_WEIGHT * jnp.trace(gram_mat) / rank_size
    inv_gram = spd_inverse(gram_mat + prox_term * jnp.eye(rank_size, dtype=jnp.float32))
    fresh_rows = jnp.dot(m_own + prox_term * old_own, inv_gram, precision=FULL_PREC, preferred_element_type=jnp.float32)
    col_sq = lax.psum(jnp.sum(fresh_rows * fresh_rows, axis=0), ALL_AXES)
    col_scale = jnp.sqrt(col_sq / total_rows)
    return fresh_rows / col_scale, col_scale


def expand_slab(own_rows, owner_axes):
    return lax.all_gather(own_rows.astype(jnp.bfloat16), owner_axes, axis=0, tiled=True)


def fold_slab(part_rows, owner_axes):
    return lax.psum_scatter(part_rows, owner_axes, scatter_dimension=0, tiled=True)


def solution(mesh):
    size_z = mesh.shape["gz"]
    size_y = mesh.shape["gy"]
    size_x = mesh.shape["gx"]
    n_dev = size_z * size_y * size_x
    owners_a = ("gz", "gy")
    owners_b = ("gz", "gx")
    owners_c = ("gy", "gx")

    def device_step(nz_vals, idx_i, idx_j, idx_k, fac_a, fac_b, fac_c):
        dim_i = fac_a.shape[0] * n_dev
        dim_j = fac_b.shape[0] * n_dev
        dim_k = fac_c.shape[0] * n_dev
        gram_b = gram_all(fac_b)
        gram_c = gram_all(fac_c)
        buf_b = expand_slab(fac_b, owners_b)
        buf_c = expand_slab(fac_c, owners_c)
        part_a = slab_product(nz_vals, idx_i, idx_j, idx_k, buf_b, buf_c, dim_i // size_x)
        out_a, _ = update_owned(fold_slab(part_a, owners_a), fac_a, gram_b, gram_c, dim_i)
        gram_a = gram_all(out_a)
        buf_a = expand_slab(out_a, owners_a)
        part_b = slab_product(nz_vals, idx_j, idx_i, idx_k, buf_a, buf_c, dim_j // size_y)
        out_b, _ = update_owned(fold_slab(part_b, owners_b), fac_b, gram_a, gram_c, dim_j)
        gram_nb = gram_all(out_b)
        buf_nb = expand_slab(out_b, owners_b)
        part_c = slab_product(nz_vals, idx_k, idx_i, idx_j, buf_a, buf_nb, dim_k // size_z)
        out_c, lambdas = update_owned(fold_slab(part_c, owners_c), fac_c, gram_a, gram_nb, dim_k)
        return out_a, out_b, out_c, lambdas

    spec_nz = P(("gz", "gy", "gx"))
    spec_a = P(("gx", "gz", "gy"), None)
    spec_b = P(("gy", "gz", "gx"), None)
    spec_c = P(("gz", "gy", "gx"), None)
    return jax.shard_map(device_step, mesh=mesh, in_specs=(spec_nz, spec_nz, spec_nz, spec_nz, spec_a, spec_b, spec_c), out_specs=(spec_a, spec_b, spec_c, P()), check_vma=False)
```

profile of v0, /device:TPU:0, one launch (start us, length us, event | category | flops | bytes accessed | tf_op | source)
XLA Modules:
  0.0 7324.8 jit_solution(9616402312983109067)
XLA Ops:
  7.2 2.0 convert_bitcast_fusion.1
  9.3 2.0 convert_element_type.38
  11.3 1.0 fusion.45
  12.4 1.0 fusion.44
  13.4 1.3 compare_and_fusion.1
  14.7 32.7 all-gather.11.cloned.1.call-done
  47.3 7.7 copy.40
  55.1 221.8 %gather_fusion = bf16[65536,64]{1,0:T(8,128)(2,1)} fusion(bf16[28160,64]{1,0:T(8,128)(2,1)} %bitcast.47, s32[65536]{0:T(1024)S(1)} %fusion.45), kind=kCustom, calls=%fused_computation.1.clone | custom fusion | bytes 17039360 | tf_op jit(solution)/shard_map/jit(_take)/gather | solution.py:18
  276.8 13.7 copy.39
  290.5 817.2 %scatter_custom_fusion = f32[75264,64]{1,0:T(8,128)} fusion(s32[65536]{0:T(1024)} %param.20, f32[]{:T(128)} %constant.333.clone.1, f32[65536]{0:T(1024)S(1)} %copy-done.6, pred[65536]{0:T(1024)(128)(4,1)S(1)} %get-tuple-element.383, bf16[]{:T(256)} %constant.309.clone.2, bf16[65536,64]{1,0:T(8,128)(2,1)} %gather_fusion, ...), kind=kCustom, calls=%fused_computation.29 | custom fusion | flops 29360128 | bytes 50856960 | tf_op jit(solution)/shard_map/scatter-add | solution.py:20
  1107.8 1.1 copy-done.2
  1108.9 0.9 fusion.54
  1109.8 0.9 fusion.55
  1110.7 1696.1 %all-reduce = (f32[64,64]{1,0:T(8,128)S(1)}, f32[64,64]{1,0:T(8,128)S(1)}) all-reduce(f32[64,64]{1,0:T(8,128)S(1)} %fusion.54, f32[64,64]{1,0:T(8,128)S(1)} %fusion.55), channel_id=1, replica_groups=mesh['gz'=4,'gy'=2,'gx'=4] {'gz','gy','gx'}, use_global_device_ids=true, to_apply=%region_2.5 | all-reduce | flops 8192 | bytes 65536 | tf_op jit(solution)/shard_map/psum | solution.py:13
  2808.3 5.0 copy.41
  2813.3 99.6 %while.51 = (s32[]{:T(128)}, f32[64,128]{0,1:T(8,128)S(1)}, s32[]{:T(128)}, s32[]{:T(128)}, s32[]{:T(128)}, /*index=5*/s32[]{:T(128)}) while((s32[]{:T(128)}, f32[64,128]{0,1:T(8,128)S(1)}, s32[]{:T(128)}, s32[]{:T(128)}, s32[]{:T(128)}, /*index=5*/s32[]{:T(128)}) %tuple.144), condition=%wide.region_6.9_spmd.clone, body=%wide.region_5.8_spmd.clone.sunk | while | flops 24772 | bytes 68097 | solution.py:35
  2815.5 0.8 fusion.69
  2913.0 460.0 %reduce-scatter.4.cloned.1.call-done = f32[9408,64]{1,0:T(8,128)} async-done(((f32[75264,64]{1,0:T(8,128)}), f32[9408,64]{1,0:T(8,128)}) %reduce-scatter.4.cloned.1.call-update) | async-done | bytes 2408464 | tf_op jit(solution)/shard_map/reduce_scatter | solution.py:55
  3373.0 10.6 multiply_reduce_fusion
  3383.6 39.6 psum.51
  3423.2 3.0 convert_bitcast_fusion
  3426.8 3.4 copy.45
  3430.1 1.7 compare_and_fusion
  3431.8 1.7 fusion.46
  3433.5 2.6 fusion.56
  3436.1 41.3 psum.52
  3477.5 2.1 select_reduce_fusion.1
  3481.7 0.8 copy.46
  3482.6 84.8 %all-gather.13.cloned.1.call-done = bf16[8,9408,64]{1,2,0:T(8,128)(2,1)} async-done(((bf16[1,9408,64]{1,2,0:T(8,128)(2,1)}), bf16[8,9408,64]{1,2,0:T(8,128)(2,1)}) %all-gather.13.cloned.1.call-update) | async-done | bytes 9633808 | tf_op jit(solution)/shard_map/all_gather | solution.py:51
  3567.4 18.2 copy.50
  3585.6 247.6 %gather_fusion.1 = bf16[65536,64]{1,0:T(8,128)(2,1)} fusion(bf16[75264,64]{1,0:T(8,128)(2,1)} %bitcast.48, s32[65536]{0:T(1024)} %fusion.46), kind=kCustom, calls=%fused_computation.2.clone | custom fusion | bytes 17039360 | tf_op jit(solution)/shard_map/jit(_take)/gather | solution.py:17
  3833.2 411.9 %scatter_custom_fusion.1 = f32[55296,64]{1,0:T(8,128)} fusion(s32[65536]{0:T(1024)} %param.21, f32[65536]{0:T(1024)S(1)} %copy-done.7, f32[]{:T(128)} %constant.333.clone.1, bf16[65536,64]{1,0:T(8,128)(2,1)} %gather_fusion, pred[65536]{0:T(1024)(128)(4,1)S(1)} %get-tuple-element.382, bf16[]{:T(256)} %constant.309.clone.2, ...), kind=kCustom, calls=%fused_computation.31 | custom fusion | flops 29360128 | bytes 48104448 | tf_op jit(solution)/shard_map/scatter-add | solution.py:20
  4245.2 99.7 %while.52 = (s32[]{:T(128)}, f32[64,128]{0,1:T(8,128)S(1)}, s32[]{:T(128)}, s32[]{:T(128)}, s32[]{:T(128)}, /*index=5*/s32[]{:T(128)}) while((s32[]{:T(128)}, f32[64,128]{0,1:T(8,128)S(1)}, s32[]{:T(128)}, s32[]{:T(128)}, s32[]{:T(128)}, /*index=5*/s32[]{:T(128)}) %tuple.147), condition=%wide.region_14.18_spmd.clone, body=%wide.region_13.17_spmd.clone.sunk | while | flops 24772 | bytes 68097 | solution.py:35
  4345.0 237.3 %reduce-scatter.6.cloned.1.call-done = f32[3456,64]{1,0:T(8,128)} async-done(((f32[55296,64]{1,0:T(8,128)}), f32[3456,64]{1,0:T(8,128)}) %reduce-scatter.6.cloned.1.call-update) | async-done | bytes 884752 | tf_op jit(solution)/shard_map/reduce_scatter | solution.py:55
  4582.3 4.7 multiply_reduce_fusion.2
  4587.0 39.4 psum.53
  4626.4 2.1 fusion.53
  4628.5 1.9 copy.48
  4630.4 0.9 fusion.57
  4631.3 41.5 psum.54
  4674.3 21.2 all-gather.9.cloned.1.call-done
  4695.5 13.7 copy.47
  4709.1 807.9 %scatter_custom_fusion.2 = f32[28160,64]{1,0:T(8,128)} fusion(s32[65536]{0:T(1024)} %param.22, f32[65536]{0:T(1024)S(1)} %copy-done.7, pred[65536]{0:T(1024)(128)(4,1)S(1)} %get-tuple-element.383, bf16[]{:T(256)} %constant.309.clone.2, f32[]{:T(128)} %constant.333.clone.1, bf16[65536,64]{1,0:T(8,128)(2,1)} %gather_fusion.1, ...), kind=kCustom, calls=%fused_computation.33 | custom fusion | flops 29360128 | bytes 38798336 | tf_op jit(solution)/shard_map/scatter-add | solution.py:20
  5517.1 99.7 %while.53 = (s32[]{:T(128)}, f32[64,128]{0,1:T(8,128)S(1)}, s32[]{:T(128)}, s32[]{:T(128)}, s32[]{:T(128)}, /*index=5*/s32[]{:T(128)}) while((s32[]{:T(128)}, f32[64,128]{0,1:T(8,128)S(1)}, s32[]{:T(128)}, s32[]{:T(128)}, s32[]{:T(128)}, /*index=5*/s32[]{:T(128)}) %tuple.150), condition=%wide.region_22.26_spmd.clone, body=%wide.region_21.25_spmd.clone.sunk | while | flops 24772 | bytes 68097 | solution.py:35
  5616.8 1653.9 %reduce-scatter.8.cloned.1.call-done = f32[3520,64]{1,0:T(8,128)} async-done(((f32[28160,64]{1,0:T(8,128)}), f32[3520,64]{1,0:T(8,128)}) %reduce-scatter.8.cloned.1.call-update) | async-done | bytes 901136 | tf_op jit(solution)/shard_map/reduce_scatter | solution.py:55
  7270.7 4.6 multiply_reduce_fusion.1
  7275.3 40.2 psum.55
  7315.5 2.2 broadcast_divide_fusion.1
  (1021 shorter events, 293.3 us)
Async XLA Ops:
  7.2 40.2 all-gather.11.cloned.1.call-start
  9.2 267.6 %all-gather.7.cloned.1.call-start = ((), (), s32[]{:S(2)}) async-start(), calls=%async_computation.3 | async-start | bytes 7520256 | tf_op jit(solution)/shard_map/all_gather | solution.py:51
  11.3 3361.7 %reduce-scatter.4.cloned.1.call-start = ((), (), s32[]{:S(2)}) async-start(), calls=%async_computation.4 | async-start | bytes 43352064 | tf_op jit(solution)/shard_map/reduce_scatter | solution.py:55
  13.4 277.1 %copy-start.8 = (s32[65536]{0:T(1024)}, s32[65536]{0:T(1024)S(1)}, u32[]{:S(2)}) copy-start(s32[65536]{0:T(1024)S(1)} %fusion.44) | copy-start | bytes 786436
  276.8 13.7 copy-start.6
  1107.7 1.2 copy-start.2
  1107.7 2.0 copy-start.1
  1107.8 2459.6 %all-gather.13.cloned.1.call-start = ((), (), s32[]{:S(2)}) async-start(), calls=%async_computation.9 | async-start | bytes 10911744 | tf_op jit(solution)/shard_map/all_gather | solution.py:51
  2806.8 1.3 copy-start.15
  2808.1 672.9 %copy-start.11 = (f32[64,64]{1,0:T(8,128)}, f32[64,64]{1,0:T(8,128)S(1)}, u32[]{:S(2)}) copy-start(f32[64,64]{1,0:T(8,128)S(1)} %fusion.50) | copy-start | bytes 49156
  3426.3 159.3 %copy-start = (f32[9408,64]{0,1:T(8,128)}, f32[9408,64]{0,1:T(8,128)S(1)}, u32[]{:S(2)}) copy-start(f32[9408,64]{0,1:T(8,128)S(1)} %get-tuple-element.373) | copy-start | bytes 7225348
  3426.3 1156.0 %reduce-scatter.6.cloned.1.call-start = ((), (), s32[]{:S(2)}) async-start(), calls=%async_computation.5 | async-start | bytes 30081024 | tf_op jit(solution)/shard_map/reduce_scatter | solution.py:55
  3477.5 3.5 copy-start.13
  3585.6 247.6 %copy-start.7 = (f32[65536]{0:T(1024)S(1)}, f32[65536]{0:T(1024)}, u32[]{:S(2)}) copy-start(f32[65536]{0:T(1024)} %param.19) | copy-start | bytes 786436
  3585.6 247.6 %copy-start.10 = (pred[65536]{0:T(1024)(128)(4,1)S(1)}, pred[65536]{0:T(1024)(128)(4,1)}, u32[]{:S(2)}) copy-start(pred[65536]{0:T(1024)(128)(4,1)} %compare_and_fusion) | copy-start | bytes 196612
  4245.1 337.1 %copy-start.5 = (f32[3456,64]{1,0:T(8,128)S(1)}, f32[3456,64]{1,0:T(8,128)}, u32[]{:S(2)}) copy-start(f32[3456,64]{1,0:T(8,128)} %copy.45) | copy-start | bytes 2654212
  4245.1 427.6 %copy-start.14 = (f32[64,64]{1,0:T(8,128)S(1)}, f32[64,64]{1,0:T(8,128)}, u32[]{:S(2)}) copy-start(f32[64,64]{1,0:T(8,128)} %copy-done.13) | copy-start | bytes 49156
  4245.2 428.9 %copy-start.12 = (f32[64,64]{1,0:T(8,128)S(1)}, f32[64,64]{1,0:T(8,128)}, u32[]{:S(2)}) copy-start(f32[64,64]{1,0:T(8,128)} %copy-done.11) | copy-start | bytes 49156
  4245.2 450.3 %all-gather.9.cloned.1.call-start = ((), (), s32[]{:S(2)}) async-start(), calls=%async_computation.6 | async-start | bytes 7520256 | tf_op jit(solution)/shard_map/all_gather | solution.py:51
  4345.0 364.2 %copy-start.9 = (s32[65536]{0:T(1024)S(1)}, s32[65536]{0:T(1024)}, u32[]{:S(2)}) copy-start(s32[65536]{0:T(1024)} %copy-done.8) | copy-start | bytes 786436
  4628.5 888.6 %copy-start.3 = (f32[3456,64]{0,1:T(8,128)}, f32[3456,64]{0,1:T(8,128)S(1)}, u32[]{:S(2)}) copy-start(f32[3456,64]{0,1:T(8,128)S(1)} %get-tuple-element.369) | copy-start | bytes 2654212
  4628.5 2642.2 %reduce-scatter.8.cloned.1.call-start = ((), (), s32[]{:S(2)}) async-start(), calls=%async_computation.7 | async-start | bytes 16220160 | tf_op jit(solution)/shard_map/reduce_scatter | solution.py:55
  5517.1 1753.6 %copy-start.4 = (f32[3520,64]{1,0:T(8,128)S(1)}, f32[3520,64]{1,0:T(8,128)}, u32[]{:S(2)}) copy-start(f32[3520,64]{1,0:T(8,128)} %copy.48) | copy-start | bytes 2703364
  7315.5 2.2 copy-start.16
Sparse Core Ops, SparseCore 0:
  10.4 36.8 all-gather.10
  50.1 65.6 all-gather.6
  1107.9 2265.0 reduce-scatter.3
  3426.4 140.9 all-gather.12
  4245.3 336.9 reduce-scatter.5
  4628.6 66.8 all-gather.8
  5517.2 1753.4 reduce-scatter.7
where the time goes:
time: 7260 us; the launch traced here: 7320 us
  waiting for transfers between devices  2490 us (34%)
  other arithmetic  2240 us (31%)
  blocking collectives  1900 us (26%)
  local copies, waits for them, and re-layouts  650 us (9%)
    reduce_scatter x3, waiting for transfers between devices, fold_slab(): lax.psum_scatter(part_rows, owner_axes, scatter_dimension=0, tiled=True)  2350 us
    scatter-add x3, other arithmetic, slab_product(): return jax.ops.segment_sum(contrib, out_rows, num_segments=slab_rows)  2040 us
    psum x3, blocking collectives, gram_all(): return lax.psum(part_gram, ALL_AXES)  1780 us
    gather x1, local copies, waits for them, and re-layouts, slab_product(): picked_one = jnp.take(buf_one, rows_one, axis=0).astype(jnp.float32)  248 us
    gather x1, local copies, waits for them, and re-layouts, slab_product(): picked_two = jnp.take(buf_two, rows_two, axis=0).astype(jnp.float32)  222 us
    div x192, other arithmetic, value_a9(): pivot_row = pivot_row / pivot_val  157 us
  transfers between devices with their start and end apart: 7, of which 6 were waited for; matrix products, arithmetic and copies ran while one was open for 8% of the time, Pallas kernels for 0%

commit v1 on v0

v1 whole, which is shorter than its diff:
```python
import functools

import jax
import jax.numpy as jnp
from jax import lax
from jax.experimental import pallas as pl
from jax.experimental.pallas import tpu as pltpu
from jax.sharding import PartitionSpec as P

HIGHEST = lax.Precision.HIGHEST
PROX_WEIGHT = 0.5
ALL_AXES = ("gz", "gy", "gx")

LANES = 128
RANK = 64
BLOCK = 1024
UNROLL = 16
STEPS = LANES // UNROLL
CHUNK = 8192
VMEM_MAX = 67_000_000


def lines_of(own_rows):
    return pl.cdiv(own_rows, 256) * 128


def place_rows(idx, own_rows):
    blk = idx // own_rows
    q = idx - blk * own_rows
    line = blk * lines_of(own_rows) + ((q >> 8) << 7) + (q & 127)
    return line, (q >> 7) & 1


def _bit(n):
    return 1 << n if n < 31 else -(1 << 31)


def mttkrp_body(
    rows_out, rows_one, rows_two, chunk, stage_rows,
    nblk_ref, flag_ref, out_h, one_h, two_h, val_ref, code_ref, line_ref, tab1_h, tab2_h, sum_h,
    acc, acc2, tab1, tab2, stage, raw1a, raw1b, raw2a, raw2b, contrib_a, contrib_b,
    sm_out, sm_one, sm_two, sem_idx, sem_tab, sem_out,
):
    raw1, raw2, contrib = (raw1a, raw1b), (raw2a, raw2b), (contrib_a, contrib_b)
    nblk = nblk_ref[0]
    blk_chunk = chunk // BLOCK
    nchunk = lax.div(nblk + (blk_chunk - 1), blk_chunk)

    def idx_copies(c, slot):
        src = pl.ds(pl.multiple_of(c * chunk, chunk), chunk)
        dst = pl.ds(pl.multiple_of(slot * chunk, chunk), chunk)
        pairs = ((out_h, sm_out), (one_h, sm_one), (two_h, sm_two))
        return [pltpu.make_async_copy(h.at[src], s.at[dst], sem_idx.at[slot, n]) for n, (h, s) in enumerate(pairs)]

    for cp in idx_copies(0, 0):
        cp.start()

    def tab_copy(tab_h, i, slot):
        src = tab_h.at[pl.ds(pl.multiple_of(i * stage_rows, stage_rows), stage_rows), :]
        return pltpu.make_async_copy(src, stage.at[slot], sem_tab.at[slot])

    tab_copy(tab1_h, 0, 0).start()

    def zero(r, _):
        at = pl.ds(pl.multiple_of(r * 128, 128), 128)
        acc[at, :] = jnp.zeros((128, LANES), jnp.float32)
        acc2[at, :] = jnp.zeros((128, LANES), jnp.float32)
        return 0

    lax.fori_loop(0, rows_out // 128, zero, 0)
    acc[pl.ds(rows_out, 16), :] = jnp.zeros((16, LANES), jnp.float32)
    acc2[pl.ds(rows_out, 16), :] = jnp.zeros((16, LANES), jnp.float32)

    def widen_table(tab_h, tab, rows, first_started):
        n = rows // stage_rows
        if not first_started:
            tab_copy(tab_h, 0, 0).start()

        def step(i, _):
            slot = lax.rem(i, 2)

            @pl.when(i + 1 < n)
            def _():
                tab_copy(tab_h, i + 1, 1 - slot).start()

            tab_copy(tab_h, i, slot).wait()

            def widen(r, _):
                at = pl.multiple_of(r * 64, 64)
                dst = pl.ds(pl.multiple_of(i * stage_rows + at, 64), 64)
                tab[dst, :] = stage[slot, pl.ds(at, 64), :].astype(jnp.float32)
                return 0

            lax.fori_loop(0, stage_rows // 64, widen, 0)
            return 0

        lax.fori_loop(0, n, step, 0)

    widen_table(tab1_h, tab1, rows_one, True)
    widen_table(tab2_h, tab2, rows_two, False)

    sub = lax.broadcasted_iota(jnp.int32, (8, LANES), 0)
    lane_id = lax.broadcasted_iota(jnp.int32, (8, LANES), 1)
    right = lane_id >= RANK
    span = 2 * chunk - (7 * 128 + UNROLL - 1)

    def at(sm, s, t):
        return sm.at[pl.ds(128 * s + t, span)]

    def pick(block, lane):
        index = jnp.full((8, LANES), lane, jnp.int32)
        return jnp.take_along_axis(block, index, axis=1, mode="promise_in_bounds")

    def rows8(tab, sm, r, t):
        x = jnp.broadcast_to(tab[pl.ds(at(sm, 0, t)[r], 1), :], (8, LANES))
        for s in range(1, 8):
            row = jnp.broadcast_to(tab[pl.ds(at(sm, s, t)[r], 1), :], (8, LANES))
            x = jnp.where(sub == s, row, x)
        return x

    def gather_group(par, r, t):
        g = slice(8 * t, 8 * t + 8)
        raw1[par][g, :] = rows8(tab1, sm_one, r, t)
        raw2[par][g, :] = rows8(tab2, sm_two, r, t)

    def product_group(par, t, vals, turns, keeps, lane0):
        g = slice(8 * t, 8 * t + 8)
        val = pick(vals, lane0 + t)
        x1, x2 = raw1[par][g, :], raw2[par][g, :]
        x1 = jnp.where((turns & _bit(t)) != 0, pltpu.roll(x1, RANK, axis=1), x1)
        x2 = jnp.where((turns & _bit(16 + t)) != 0, pltpu.roll(x2, RANK, axis=1), x2)
        contrib[par][g, :] = jnp.where((keeps & _bit(t)) != 0, val * (x1 * x2), 0.0)

    def add_group(par, r, t):
        x = contrib[par][8 * t : 8 * t + 8, :]
        row = [at(sm_out, s, t)[r] for s in range(8)]
        dst = acc if t % 2 == 0 else acc2
        sums = [dst[pl.ds(row[s], 8), :] + x for s in range(8)]
        for s in range(8):
            pltpu.store(dst.at[pl.ds(row[s], 8), :], sums[s], mask=(sub == s))

    def merge(par, b, q, flag):
        lines = line_ref[pl.ds(pl.multiple_of(b * 8, 8), 8), :] + sub

        def one(t, _):
            @pl.when((lax.shift_right_logical(flag, t) & 1) == 1)
            def _():
                line = pick(lines, q * UNROLL + t)
                rows = pl.ds(pl.multiple_of(t * 8, 8), 8)
                y = contrib[par][rows, :]
                total = y
                for d in range(1, 8):
                    same = (line == pltpu.roll(line, d, axis=0)) & (sub >= d)
                    total = total + jnp.where(same, pltpu.roll(y, d, axis=0), 0.0)
                contrib[par][rows, :] = total

            return 0

        lax.fori_loop(0, UNROLL, one, 0)

    def chunk_step(c, _):
        slot = lax.rem(c, 2)
        for cp in idx_copies(c, slot):
            cp.wait()

        @pl.when(c + 1 < nchunk)
        def _():
            for cp in idx_copies(c + 1, 1 - slot):
                cp.start()

        n_it = jnp.minimum(blk_chunk, nblk - c * blk_chunk) * STEPS
        last = n_it - 1
        base = slot * chunk

        def place(k):
            bl = k // STEPS
            q = k - bl * STEPS
            return c * blk_chunk + bl, q, base + bl * BLOCK + q * UNROLL

        def block_of(ref, b):
            return ref[pl.ds(pl.multiple_of(b * 8, 8), 8), :]

        def front(k):
            b, q, _ = place(jnp.minimum(k, last))
            codes = block_of(code_ref, b)
            keeps = pick(codes, q + STEPS)
            return block_of(val_ref, b), pick(codes, q), jnp.where(right, keeps, ~keeps), q * UNROLL

        def fetch(par, k):
            _, _, r = place(jnp.minimum(k, last))
            for t in range(UNROLL):
                gather_group(par, r, t)

        fetch(0, 0)
        args0 = front(0)
        for t in range(UNROLL):
            product_group(0, t, *args0)
        fetch(1, 1)

        def step(j, _):
            for par in range(2):
                k = 2 * j + par
                b, q, r = place(k)
                flag = flag_ref[c * (blk_chunk * STEPS) + k]

                @pl.when(flag != 0)
                def _():
                    merge(par, b, q, flag)

                args = front(k + 1)
                _, _, rn = place(jnp.minimum(k + 2, last))
                for t in range(UNROLL):
                    add_group(par, r, t)
                    product_group(1 - par, t, *args)
                    gather_group(par, rn, t)
            return 0

        lax.fori_loop(0, lax.div(n_it, 2), step, 0)
        return 0

    lax.fori_loop(0, nchunk, chunk_step, 0)

    def total(r, _):
        rows = pl.ds(pl.multiple_of(r * 64 + 8, 8), 64)
        acc[rows, :] = acc[rows, :] + acc2[rows, :]
        return 0

    lax.fori_loop(0, rows_out // 64, total, 0)
    cp = pltpu.make_async_copy(acc.at[pl.ds(8, rows_out), :], sum_h, sem_out)
    cp.start()
    cp.wait()


def mttkrp(name, plan, tab1, tab2, rows_out):
    nblk, flags, line_out, line_one, line_two, vals, code = plan
    nnz = line_out.shape[0]
    rows_one, rows_two = tab1.shape[0], tab2.shape[0]
    chunk = min(CHUNK, nnz)
    stage_rows = 896 if rows_one % 896 == 0 and rows_two % 896 == 0 else 128
    smem = pl.BlockSpec(memory_space=pltpu.SMEM)
    anym = pl.BlockSpec(memory_space=pl.ANY)
    vmem = pl.BlockSpec(memory_space=pltpu.VMEM)
    tiles = (nnz // LANES, LANES)
    step_buf = pltpu.VMEM((8 * UNROLL, LANES), jnp.float32)
    return pl.pallas_call(
        functools.partial(mttkrp_body, rows_out, rows_one, rows_two, chunk, stage_rows),
        out_shape=jax.ShapeDtypeStruct((rows_out, LANES), jnp.float32),
        in_specs=[smem, smem, anym, anym, anym, vmem, vmem, vmem, anym, anym],
        out_specs=anym,
        scratch_shapes=[
            pltpu.VMEM((rows_out + 16, LANES), jnp.float32),
            pltpu.VMEM((rows_out + 16, LANES), jnp.float32),
            pltpu.VMEM((rows_one, LANES), jnp.float32),
            pltpu.VMEM((rows_two, LANES), jnp.float32),
            pltpu.VMEM((2, stage_rows, LANES), jnp.bfloat16),
            *([step_buf] * 6),
            pltpu.SMEM((2 * chunk,), jnp.int32),
            pltpu.SMEM((2 * chunk,), jnp.int32),
            pltpu.SMEM((2 * chunk,), jnp.int32),
            pltpu.SemaphoreType.DMA((2, 3)),
            pltpu.SemaphoreType.DMA((2,)),
            pltpu.SemaphoreType.DMA,
        ],
        name=name,
        compiler_params=pltpu.CompilerParams(vmem_limit_bytes=VMEM_MAX),
        cost_estimate=pl.CostEstimate(flops=2_000_000_000, bytes_accessed=50_000_000, transcendentals=0),
    )(nblk, flags, line_out, line_one, line_two, vals.reshape(tiles), code, line_out.reshape(tiles), tab1, tab2)


def plan_mode(nblk, nz_vals, out_place, one_place, two_place, rows_out):
    nnz = nz_vals.shape[0]
    shape = (nnz // BLOCK, 8, LANES)
    sub = lax.broadcasted_iota(jnp.int32, shape, 1)
    line = jnp.where(nz_vals != 0, out_place[0], rows_out).reshape(shape)
    repeated = jnp.zeros((shape[0], LANES), jnp.bool_)
    for d in range(1, 8):
        same = (line[:, d:] == line[:, : 8 - d]) & (line[:, d:] != rows_out)
        repeated = repeated | jnp.any(same, axis=1)
    lane = jnp.arange(LANES)
    powers = jnp.where(lane[:, None] // UNROLL == jnp.arange(STEPS)[None, :], 1 << (lane[:, None] % UNROLL), 0)

    def words(bits):
        out = jnp.dot(bits.astype(jnp.bfloat16), powers.astype(jnp.bfloat16), preferred_element_type=jnp.float32)
        return out.astype(jnp.int32)

    rows = (nnz // LANES, LANES)
    half = out_place[1].reshape(rows)
    turn_one = words(one_place[1].reshape(rows) ^ half)
    turn_two = words(two_place[1].reshape(rows) ^ half)
    pad = jnp.zeros((rows[0], LANES - 2 * STEPS), jnp.int32)
    code = jnp.concatenate([turn_one | (turn_two << 16), words(half), pad], axis=1)
    flags = words(repeated).reshape(-1)
    return nblk, flags, (line + 8 - sub).reshape(nnz), one_place[0], two_place[0], nz_vals, code


def dot_t(a, b, dims):
    return lax.dot_general(a, b, (dims, ((), ())), precision=HIGHEST, preferred_element_type=jnp.float32)


def col_tiles(width, body, tail):
    full = width // 256
    if full:
        lax.fori_loop(0, full, lambda t, _: (body(t), 0)[1], 0)
    if width % 256:
        tail(full, width % 256)


def pack_tile(x, out_ref, t):
    w = x.shape[1]
    if w < 256:
        x = jnp.concatenate([x, jnp.zeros((RANK, 256 - w), jnp.float32)], axis=1)
    both = jnp.concatenate([x[:, :128], x[:, 128:]], axis=0)
    at = t * 128 if isinstance(t, int) else pl.multiple_of(t * 128, 128)
    out_ref[pl.ds(at, 128), :] = both.T.astype(jnp.bfloat16)


def cols(ref, t, w):
    at = t * 256 if isinstance(t, int) else pl.multiple_of(t * 256, 256)
    return ref.at[:, pl.ds(at, w)]


def prep_body(b_ref, c_ref, pack_b, pack_c, gram_b, gram_c):
    for src, pack, gram in ((b_ref, pack_b, gram_b), (c_ref, pack_c, gram_c)):
        gram[...] = jnp.zeros((RANK, RANK), jnp.float32)

        def tile(t, w, src=src, pack=pack, gram=gram):
            x = cols(src, t, w)[...]
            pack_tile(x, pack, t)
            gram[...] += dot_t(x, x, ((1,), (1,)))

        col_tiles(src.shape[1], lambda t: tile(t, 256), tile)


def prep(fac_b_t, fac_c_t):
    packs = [jax.ShapeDtypeStruct((lines_of(f.shape[1]), LANES), jnp.bfloat16) for f in (fac_b_t, fac_c_t)]
    gram = jax.ShapeDtypeStruct((RANK, RANK), jnp.float32)
    return pl.pallas_call(prep_body, out_shape=(*packs, gram, gram), name="prep")(fac_b_t, fac_c_t)


def invert_body(g1_ref, g2_ref, inv_ref, mu_ref, aug):
    order = RANK
    gram = g1_ref[...] * g2_ref[...]
    row_id = lax.broadcasted_iota(jnp.int32, (order, order), 0)
    col_id = lax.broadcasted_iota(jnp.int32, (order, order), 1)
    diag = row_id == col_id
    mu = PROX_WEIGHT * jnp.sum(jnp.where(diag, gram, 0.0), keepdims=True) / order
    mu_ref[...] = jnp.broadcast_to(mu, (8, LANES))
    eye = jnp.where(diag, 1.0, 0.0)
    aug[...] = jnp.concatenate([gram + mu * eye, eye], axis=1)
    rows = lax.broadcasted_iota(jnp.int32, (order, 2 * order), 0)
    lanes = lax.broadcasted_iota(jnp.int32, (order, 2 * order), 1)

    def eliminate(p, _):
        full = aug[...]
        row = aug[pl.ds(p, 1), :]
        col = jnp.sum(jnp.where(lanes == p, full, 0.0), axis=1, keepdims=True)
        pivot = jnp.sum(jnp.where(lanes[:1] == p, row, 0.0), axis=1, keepdims=True)
        row = row / pivot
        aug[...] = jnp.where(rows == p, row, full - col * row)
        return 0

    lax.fori_loop(0, order, eliminate, 0)
    inv_ref[...] = aug[:, order:]


def invert(name, gram_one, gram_two):
    return pl.pallas_call(
        invert_body,
        out_shape=(jax.ShapeDtypeStruct((RANK, RANK), jnp.float32), jax.ShapeDtypeStruct((8, LANES), jnp.float32)),
        scratch_shapes=[pltpu.VMEM((RANK, 2 * RANK), jnp.float32)],
        name=name,
    )(gram_one, gram_two)


def solve_body(m_ref, old_ref, inv_ref, mu_ref, fresh_ref, gram_ref):
    gram_ref[...] = jnp.zeros((RANK, RANK), jnp.float32)
    inv = inv_ref[...]
    mu = mu_ref[:1, :1]

    def tile(t, w):
        at = t * 128 if isinstance(t, int) else pl.multiple_of(t * 128, 128)
        m = m_ref[pl.ds(at, 128), :].T
        m = jnp.concatenate([m[:RANK], m[RANK:]], axis=1)[:, :w]
        y = m + mu * cols(old_ref, t, w)[...]
        x = dot_t(inv, y, ((0,), (0,)))
        cols(fresh_ref, t, w)[...] = x
        gram_ref[...] += dot_t(x, x, ((1,), (1,)))

    col_tiles(old_ref.shape[1], lambda t: tile(t, 256), tile)


def solve(name, m_own, old_t, inv, mu):
    return pl.pallas_call(
        solve_body,
        out_shape=(jax.ShapeDtypeStruct(old_t.shape, jnp.float32), jax.ShapeDtypeStruct((RANK, RANK), jnp.float32)),
        name=name,
    )(m_own, old_t, inv, mu)


def scale_body(total_rows, want_pack, fresh_ref, gram_ref, out_ref, lam_ref, scaled_ref, *pack_ref):
    gram = gram_ref[...]
    row_id = lax.broadcasted_iota(jnp.int32, (RANK, RANK), 0)
    col_id = lax.broadcasted_iota(jnp.int32, (RANK, RANK), 1)
    square = jnp.where(row_id == col_id, gram, 0.0)
    lam_col = jnp.sqrt(jnp.sum(square, axis=1, keepdims=True) / total_rows)
    lam_row = jnp.sqrt(jnp.sum(square, axis=0, keepdims=True) / total_rows)
    lam_ref[...] = lam_row
    scaled_ref[...] = gram / lam_col / lam_row

    def tile(t, w):
        x = cols(fresh_ref, t, w)[...] / lam_col
        cols(out_ref, t, w)[...] = x
        if want_pack:
            pack_tile(x, pack_ref[0], t)

    col_tiles(fresh_ref.shape[1], lambda t: tile(t, 256), tile)


def scale(name, fresh_t, gram_sum, total_rows, want_pack):
    own = fresh_t.shape[1]
    outs = [
        jax.ShapeDtypeStruct(fresh_t.shape, jnp.float32),
        jax.ShapeDtypeStruct((1, RANK), jnp.float32),
        jax.ShapeDtypeStruct((RANK, RANK), jnp.float32),
    ]
    if want_pack:
        outs.append(jax.ShapeDtypeStruct((lines_of(own), LANES), jnp.bfloat16))
    return pl.pallas_call(functools.partial(scale_body, total_rows, want_pack), out_shape=tuple(outs), name=name)(fresh_t, gram_sum)


def expand_slab(own_lines, owner_axes):
    return lax.all_gather(own_lines, owner_axes, axis=0, tiled=True)


def fold_slab(part_lines, owner_axes):
    return lax.psum_scatter(part_lines, owner_axes, scatter_dimension=0, tiled=True)


def solution(mesh):
    size_z = mesh.shape["gz"]
    size_y = mesh.shape["gy"]
    size_x = mesh.shape["gx"]
    n_dev = size_z * size_y * size_x
    owners_a = ("gz", "gy")
    owners_b = ("gz", "gx")
    owners_c = ("gy", "gx")

    def device_step(nz_vals, idx_i, idx_j, idx_k, fac_a, fac_b, fac_c):
        own_a, own_b, own_c = fac_a.shape[0], fac_b.shape[0], fac_c.shape[0]
        rows_a = lines_of(own_a) * (n_dev // size_x)
        rows_b = lines_of(own_b) * (n_dev // size_y)
        rows_c = lines_of(own_c) * (n_dev // size_z)
        old_a, old_b, old_c = fac_a.T, fac_b.T, fac_c.T

        pack_b, pack_c, gram_b, gram_c = prep(old_b, old_c)
        gram_b, gram_c = lax.psum((gram_b, gram_c), ALL_AXES)
        buf_b = expand_slab(pack_b, owners_b)
        buf_c = expand_slab(pack_c, owners_c)

        at_a = place_rows(idx_i, own_a)
        at_b = place_rows(idx_j, own_b)
        at_c = place_rows(idx_k, own_c)
        used = jnp.max(jnp.where(nz_vals != 0, jnp.arange(nz_vals.shape[0], dtype=jnp.int32) + 1, 1))
        nblk = ((used + (BLOCK - 1)) // BLOCK).reshape(1)

        plan_a = plan_mode(nblk, nz_vals, at_a, at_b, at_c, rows_a)
        part_a = mttkrp("mttkrp_a", plan_a, buf_b, buf_c, rows_a)
        inv, mu = invert("invert_a", gram_b, gram_c)
        fresh, gram = solve("solve_a", fold_slab(part_a, owners_a), old_a, inv, mu)
        out_a, _, gram_a, pack_a = scale("scale_a", fresh, lax.psum(gram, ALL_AXES), own_a * n_dev, True)
        buf_a = expand_slab(pack_a, owners_a)

        plan_b = plan_mode(nblk, nz_vals, at_b, at_a, at_c, rows_b)
        part_b = mttkrp("mttkrp_b", plan_b, buf_a, buf_c, rows_b)
        inv, mu = invert("invert_b", gram_a, gram_c)
        fresh, gram = solve("solve_b", fold_slab(part_b, owners_b), old_b, inv, mu)
        out_b, _, gram_nb, pack_nb = scale("scale_b", fresh, lax.psum(gram, ALL_AXES), own_b * n_dev, True)
        buf_nb = expand_slab(pack_nb, owners_b)

        plan_c = plan_mode(nblk, nz_vals, at_c, at_a, at_b, rows_c)
        part_c = mttkrp("mttkrp_c", plan_c, buf_a, buf_nb, rows_c)
        inv, mu = invert("invert_c", gram_a, gram_nb)
        fresh, gram = solve("solve_c", fold_slab(part_c, owners_c), old_c, inv, mu)
        out_c, lambdas, _ = scale("scale_c", fresh, lax.psum(gram, ALL_AXES), own_c * n_dev, False)
        return out_a.T, out_b.T, out_c.T, lambdas.reshape(RANK)

    spec_nz = P(("gz", "gy", "gx"))
    spec_a = P(("gx", "gz", "gy"), None)
    spec_b = P(("gy", "gz", "gx"), None)
    spec_c = P(("gz", "gy", "gx"), None)
    return jax.shard_map(
        device_step,
        mesh=mesh,
        in_specs=(spec_nz, spec_nz, spec_nz, spec_nz, spec_a, spec_b, spec_c),
        out_specs=(spec_a, spec_b, spec_c, P()),
        check_vma=False,
    )
```

time: 7260 us -> 1940 us (0.27); the launches traced: 7320 us -> 1910 us
  other arithmetic: 2240 us -> 10.1 us
  blocking collectives: 1900 us -> 161 us
  waiting for transfers between devices: 2490 us -> 752 us
  Pallas kernels: 0 us -> 961 us
  local copies, waits for them, and re-layouts: 650 us -> 4.36 us
    scatter-add x3 -> x0, other arithmetic: 2040 us -> none  [slab_product(): return jax.ops.segment_sum(contrib, out_rows, num_segments=slab_rows)]
    reduce_scatter x3, waiting for transfers between devices: 2350 us -> 456 us  [fold_slab(): lax.psum_scatter(part_lines, owner_axes, scatter_dimension=0, tiled=True)]
    psum x6 -> x4, blocking collectives: 1900 us -> 161 us  [the longest x3 121 us: device_step(): lax.psum(gram, ALL_AXES)]
    pallas_call x0 -> x13, Pallas kernels: none -> 961 us  [the longest x3 874 us: mttkrp(): pl.pallas_call(functools.partial(mttkrp_body, rows_out, rows_one, rows_tw...]
    gather x2 -> x0, local copies, waits for them, and re-layouts: 469 us -> none  [the longest x1 248 us: slab_product(): picked_one = jnp.take(buf_one, rows_one, axis=0).astype(jnp.float32)]
    div x193 -> x0, other arithmetic: 159 us -> none  [the longest x192 157 us: value_a9(): pivot_row = pivot_row / pivot_val]
    all_gather x4, waiting for transfers between devices: 139 us -> 295 us  [expand_slab(): return lax.all_gather(own_lines, owner_axes, axis=0, tiled=True)]
    dynamic_slice x192 -> x0, local copies, waits for them, and re-layouts: 113 us -> none  [value_a9(): pivot_val = lax.dynamic_slice_in_dim(pivot_row, pivot_idx, 1, axis=1)]
  transfers between devices with their start and end apart: 7 -> 7, of which waited for: 6 -> 7; matrix products, arithmetic and copies ran while one was open for 8% -> 1% of each run, Pallas kernels for 0% -> 1%
where the time goes in v1:
time: 1940 us; the launch traced here: 1910 us
  Pallas kernels  961 us (50%)
  waiting for transfers between devices  752 us (39%)
  blocking collectives  161 us (8%)
    pallas_call x3, Pallas kernels, mttkrp(): pl.pallas_call(functools.partial(mttkrp_body, rows_out, rows_one, rows_tw...  874 us
    reduce_scatter x3, waiting for transfers between devices, fold_slab(): lax.psum_scatter(part_lines, owner_axes, scatter_dimension=0, tiled=True)  456 us
    all_gather x4, waiting for transfers between devices, expand_slab(): return lax.all_gather(own_lines, owner_axes, axis=0, tiled=True)  295 us
    psum x3, blocking collectives, device_step(): lax.psum(gram, ALL_AXES)  121 us
    pallas_call x3, Pallas kernels, solve(): pl.pallas_call(solve_body, out_shape=(jax.ShapeDtypeStruct(old_t.shape, j...  43.4 us
    psum x1, blocking collectives, device_step(): gram_b, gram_c = lax.psum((gram_b, gram_c), ALL_AXES)  40 us
  transfers between devices with their start and end apart: 7, of which 7 were waited for; matrix products, arithmetic and copies ran while one was open for 1% of the time, Pallas kernels for 1%

profile of v1, /device:TPU:0, one launch (start us, length us, event | category | flops | bytes accessed | tf_op | source)
XLA Modules:
  0.0 1907.5 jit_solution(5141040921769539272)
XLA Ops:
  7.2 7.9 prep.1
  15.2 0.7 all-gather.5.cloned.1.call-update
  16.1 2.1 bitcast_subtract_fusion
  18.2 2.5 bitcast_subtract_fusion.1
  20.6 0.7 copy-done.2
  21.3 1.8 bitcast_subtract_fusion.3
  23.9 0.4 convolution_convert_fusion.2
  24.4 0.4 convolution_convert_fusion.3
  25.0 0.4 convolution_convert_fusion.4
  25.5 0.6 convolution_convert_fusion.5
  26.6 0.1 fusion.60
  26.8 0.1 fusion.59
  27.1 0.2 convolution_convert_fusion.8
  27.5 0.6 reshape.132.flag_ref
  28.1 0.6 fusion
  28.7 0.6 fusion.128
  29.3 1.1 add_add_fusion.2
  30.4 21.8 %all-gather.7.cloned.1.call-done.tab2_h = bf16[14336,128]{1,0:T(8,128)(2,1)} async-done(((bf16[1792,128]{1,0:T(8,128)(2,1)}), bf16[14336,128]{1,0:T(8,128)(2,1)}) %all-gather.7.cloned.1.call-update) | async-done | bytes 3670032 | tf_op jit(solution)/shard_map/all_gather | solution.py:432
  52.2 70.2 %all-gather.5.cloned.1.call-done.tab1_h = bf16[28672,128]{1,0:T(8,128)(2,1)} async-done(((bf16[1792,128]{1,0:T(8,128)(2,1)}), bf16[28672,128]{1,0:T(8,128)(2,1)}) %all-gather.5.cloned.1.call-update) | async-done | bytes 7340048 | tf_op jit(solution)/shard_map/all_gather | solution.py:432
  122.4 191.5 %mttkrp_a.1 = f32[37888,128]{1,0:T(8,128)} custom-call(s32[1]{0:T(128)} %bitcast.nblk_ref, s32[512]{0:T(512)} %reshape.132.flag_ref, s32[65536]{0:T(1024)} %get-tuple-element.75.out_h, s32[65536]{0:T(1024)} %copy-done.2, s32[65536]{0:T(1024)} %copy-done.4, f32[512,128]{1,0:T(8,128)} %bitcast.54, s32[512,128]{1,0:T(8,128)} %get-tuple-element.79.code_ref, ...), custom_call_target="tpu_custom_call" | custom-call | flops 2000000000 | bytes 50000000 | tf_op jit(solution)/shard_map/mttkrp_a/pallas_call | solution.py:245
  314.0 0.7 copy-done.8
  314.7 40.0 %all-reduce = (f32[64,64]{1,0:T(8,128)}, f32[64,64]{1,0:T(8,128)}) all-reduce(f32[64,64]{1,0:T(8,128)S(1)} %copy-done.8, f32[64,64]{1,0:T(8,128)S(1)} %copy-done.9), channel_id=1, replica_groups=mesh['gz'=4,'gy'=2,'gx'=4] {'gz','gy','gx'}, use_global_device_ids=true, to_apply=%region_8.9 | all-reduce | flops 8192 | bytes 65536 | tf_op jit(solution)/shard_map/psum | solution.py:456
  354.7 7.6 invert_a.1
  362.3 264.7 %reduce-scatter.4.cloned.1.call-done.m_ref = f32[4736,128]{1,0:T(8,128)} async-done(((f32[37888,128]{1,0:T(8,128)}), f32[4736,128]{1,0:T(8,128)}) %reduce-scatter.4.cloned.1.call-update) | async-done | bytes 2424848 | tf_op jit(solution)/shard_map/reduce_scatter | solution.py:436
  627.1 23.9 %solve_a.1 = (f32[64,9408]{1,0:T(8,128)}, f32[64,64]{1,0:T(8,128)}) custom-call(f32[4736,128]{1,0:T(8,128)} %reduce-scatter.4.cloned.1.call-done.m_ref, f32[64,9408]{1,0:T(8,128)} %bitcast.61, f32[64,64]{1,0:T(8,128)} %get-tuple-element.32.inv_ref, f32[8,128]{1,0:T(8,128)} %get-tuple-element.33.mu_ref), custom_call_target="tpu_custom_call" | custom-call | tf_op jit(solution)/shard_map/solve_a/pallas_call | solution.py:393
  650.9 40.4 %psum.37.gram_ref = f32[64,64]{1,0:T(8,128)} all-reduce(f32[64,64]{1,0:T(8,128)} %get-tuple-element.35), channel_id=1, replica_groups=mesh['gz'=4,'gy'=2,'gx'=4] {'gz','gy','gx'}, use_global_device_ids=true, to_apply=%region_10.11 | all-reduce | flops 4096 | bytes 32768 | tf_op jit(solution)/shard_map/psum | solution.py:470
  691.3 7.3 scale_a.1
  698.9 0.1 fusion.17
  699.6 0.2 convolution_convert_fusion.7
  700.0 0.7 reshape.135.flag_ref
  700.7 138.1 %all-gather.9.cloned.1.call-done.tab1_h = bf16[37888,128]{1,0:T(8,128)(2,1)} async-done(((bf16[4736,128]{1,0:T(8,128)(2,1)}), bf16[37888,128]{1,0:T(8,128)(2,1)}) %all-gather.9.cloned.1.call-update) | async-done | bytes 9699344 | tf_op jit(solution)/shard_map/all_gather | solution.py:432
  838.7 320.0 %mttkrp_b.1 = f32[28672,128]{1,0:T(8,128)} custom-call(s32[1]{0:T(128)} %bitcast.nblk_ref, s32[512]{0:T(512)} %reshape.135.flag_ref, s32[65536]{0:T(1024)} %get-tuple-element.73.out_h, s32[65536]{0:T(1024)} %copy-done.3, s32[65536]{0:T(1024)} %copy-done.4, f32[512,128]{1,0:T(8,128)} %bitcast.55, s32[512,128]{1,0:T(8,128)} %get-tuple-element.78.code_ref, ...), custom_call_target="tpu_custom_call" | custom-call | flops 2000000000 | bytes 50000000 | tf_op jit(solution)/shard_map/mttkrp_b/pallas_call | solution.py:245
  1158.8 0.2 all-gather.11.cloned.1.call-start
  1159.0 7.6 invert_b.1
  1166.7 136.4 %reduce-scatter.6.cloned.1.call-done.m_ref = f32[1792,128]{1,0:T(8,128)} async-done(((f32[28672,128]{1,0:T(8,128)}), f32[1792,128]{1,0:T(8,128)}) %reduce-scatter.6.cloned.1.call-update) | async-done | bytes 917520 | tf_op jit(solution)/shard_map/reduce_scatter | solution.py:436
  1303.0 9.7 solve_b.1
  1312.7 40.7 %psum.38.gram_ref = f32[64,64]{1,0:T(8,128)} all-reduce(f32[64,64]{1,0:T(8,128)} %get-tuple-element.42), channel_id=1, replica_groups=mesh['gz'=4,'gy'=2,'gx'=4] {'gz','gy','gx'}, use_global_device_ids=true, to_apply=%region_18.19 | all-reduce | flops 4096 | bytes 32768 | tf_op jit(solution)/shard_map/psum | solution.py:477
  1353.5 3.6 scale_b.1
  1357.7 0.1 fusion.55
  1358.0 0.2 convolution_convert_fusion.6
  1358.4 0.7 reshape.137.flag_ref
  1359.1 65.1 %all-gather.11.cloned.1.call-done.tab2_h = bf16[28672,128]{1,0:T(8,128)(2,1)} async-done(((bf16[1792,128]{1,0:T(8,128)(2,1)}), bf16[28672,128]{1,0:T(8,128)(2,1)}) %all-gather.11.cloned.1.call-update) | async-done | bytes 7340048 | tf_op jit(solution)/shard_map/all_gather | solution.py:432
  1424.2 362.0 %mttkrp_c.1 = f32[14336,128]{1,0:T(8,128)} custom-call(s32[1]{0:T(128)} %bitcast.nblk_ref, s32[512]{0:T(512)} %reshape.137.flag_ref, s32[65536]{0:T(1024)} %get-tuple-element.61.out_h, s32[65536]{0:T(1024)} %copy-done.3, s32[65536]{0:T(1024)} %copy-done.2, f32[512,128]{1,0:T(8,128)} %bitcast.56, s32[512,128]{1,0:T(8,128)} %get-tuple-element.77.code_ref, ...), custom_call_target="tpu_custom_call" | custom-call | flops 2000000000 | bytes 50000000 | tf_op jit(solution)/shard_map/mttkrp_c/pallas_call | solution.py:245
  1786.2 7.6 invert_c.1
  1793.8 54.6 %reduce-scatter.8.cloned.1.call-done.m_ref = f32[1792,128]{1,0:T(8,128)} async-done(((f32[14336,128]{1,0:T(8,128)}), f32[1792,128]{1,0:T(8,128)}) %reduce-scatter.8.cloned.1.call-update) | async-done | bytes 917520 | tf_op jit(solution)/shard_map/reduce_scatter | solution.py:436
  1848.4 9.8 solve_c.1
  1858.2 40.1 %psum.39.gram_ref = f32[64,64]{1,0:T(8,128)} all-reduce(f32[64,64]{1,0:T(8,128)} %get-tuple-element.49), channel_id=1, replica_groups=mesh['gz'=4,'gy'=2,'gx'=4] {'gz','gy','gx'}, use_global_device_ids=true, to_apply=%region_26.27 | all-reduce | flops 4096 | bytes 32768 | tf_op jit(solution)/shard_map/psum | solution.py:484
  1898.3 2.3 scale_c.1
  (59 shorter events, 3.5 us)
Async XLA Ops:
  7.2 16.7 copy-start.6
  7.2 17.2 copy-start.5
  7.2 17.8 copy-start.7
  7.2 45.0 %all-gather.7.cloned.1.call-start = ((), (), s32[]{:S(2)}) async-start(), calls=%async_computation.4 | async-start | bytes 4128768 | tf_op jit(solution)/shard_map/all_gather | solution.py:432
  15.2 107.2 %all-gather.5.cloned.1.call-start = ((), (), s32[]{:S(2)}) async-start(), calls=%async_computation.3 | async-start | bytes 7798784 | tf_op jit(solution)/shard_map/all_gather | solution.py:432
  15.9 611.1 %reduce-scatter.4.cloned.1.call-start = ((), (), s32[]{:S(2)}) async-start(), calls=%async_computation.5 | async-start | bytes 21823488 | tf_op jit(solution)/shard_map/reduce_scatter | solution.py:436
  18.2 5.0 copy-start.4
  20.6 0.7 copy-start.2
  20.6 2.5 copy-start.3
  313.9 0.8 copy-start.8
  314.0 0.8 copy-start.9
  314.0 384.8 %copy-start.1 = (s32[64,8,128]{2,1,0:T(8,128)S(1)}, s32[64,8,128]{2,1,0:T(8,128)}, u32[]{:S(2)}) copy-start(s32[64,8,128]{2,1,0:T(8,128)} %get-tuple-element.72) | copy-start | bytes 786436
  314.0 524.7 %all-gather.9.cloned.1.call-start = ((), (), s32[]{:S(2)}) async-start(), calls=%async_computation.6 | async-start | bytes 10911744 | tf_op jit(solution)/shard_map/all_gather | solution.py:432
  698.7 604.3 %reduce-scatter.6.cloned.1.call-start = ((), (), s32[]{:S(2)}) async-start(), calls=%async_computation.7 | async-start | bytes 15597568 | tf_op jit(solution)/shard_map/reduce_scatter | solution.py:436
  1158.8 198.4 %copy-start = (s32[64,8,128]{2,1,0:T(8,128)S(1)}, s32[64,8,128]{2,1,0:T(8,128)}, u32[]{:S(2)}) copy-start(s32[64,8,128]{2,1,0:T(8,128)} %get-tuple-element.62) | copy-start | bytes 786436
  1158.8 265.4 %all-gather.11.cloned.1.call-start = ((), (), s32[]{:S(2)}) async-start(), calls=%async_computation.8 | async-start | bytes 7798784 | tf_op jit(solution)/shard_map/all_gather | solution.py:432
  1357.1 491.3 %reduce-scatter.8.cloned.1.call-start = ((), (), s32[]{:S(2)}) async-start(), calls=%async_computation.9 | async-start | bytes 8257536 | tf_op jit(solution)/shard_map/reduce_scatter | solution.py:436
Sparse Core Ops, SparseCore 0:
  15.3 36.8 all-gather.6
  55.1 67.2 all-gather.4
  314.1 312.9 reduce-scatter.3
  698.8 139.8 all-gather.8
  1158.9 144.0 reduce-scatter.5
  1357.2 66.8 all-gather.10
  1786.3 62.0 reduce-scatter.7

commit v2 on v1

--- a/solution.py
+++ b/solution.py
@@ -9,7 +9,6 @@
 
 HIGHEST = lax.Precision.HIGHEST
 PROX_WEIGHT = 0.5
-ALL_AXES = ("gz", "gy", "gx")
 
 LANES = 128
 RANK = 64
@@ -18,6 +17,11 @@
 STEPS = LANES // UNROLL
 CHUNK = 8192
 VMEM_MAX = 67_000_000
+TAB_STEPS = 8
+TAB_SLOTS = 3
+OUT_STEPS = 8
+WIDEN_ROWS = 32
+GATHER_PARTS = 2
 
 
 def lines_of(own_rows):
@@ -36,7 +40,7 @@
 
 
 def mttkrp_body(
-    rows_out, rows_one, rows_two, chunk, stage_rows,
+    rows_out, rows_one, rows_two, chunk,
     nblk_ref, flag_ref, out_h, one_h, two_h, val_ref, code_ref, line_ref, tab1_h, tab2_h, sum_h,
     acc, acc2, tab1, tab2, stage, raw1a, raw1b, raw2a, raw2b, contrib_a, contrib_b,
     sm_out, sm_one, sm_two, sem_idx, sem_tab, sem_out,
@@ -55,11 +59,15 @@
     for cp in idx_copies(0, 0):
         cp.start()
 
-    def tab_copy(tab_h, i, slot):
-        src = tab_h.at[pl.ds(pl.multiple_of(i * stage_rows, stage_rows), stage_rows), :]
-        return pltpu.make_async_copy(src, stage.at[slot], sem_tab.at[slot])
-
-    tab_copy(tab1_h, 0, 0).start()
+    tabs = ((tab1_h, tab1, rows_one // TAB_STEPS), (tab2_h, tab2, rows_two // TAB_STEPS))
+
+    def tab_copy(n):
+        tab_h, _, step_rows = tabs[n // TAB_STEPS]
+        src = tab_h.at[pl.ds((n % TAB_STEPS) * step_rows, step_rows), :]
+        return pltpu.make_async_copy(src, stage.at[n % TAB_SLOTS, pl.ds(0, step_rows), :], sem_tab.at[n % TAB_SLOTS])
+
+    for n in range(TAB_SLOTS):
+        tab_copy(n).start()
 
     def zero(r, _):
         at = pl.ds(pl.multiple_of(r * 128, 128), 128)
@@ -71,33 +79,19 @@
     acc[pl.ds(rows_out, 16), :] = jnp.zeros((16, LANES), jnp.float32)
     acc2[pl.ds(rows_out, 16), :] = jnp.zeros((16, LANES), jnp.float32)
 
-    def widen_table(tab_h, tab, rows, first_started):
-        n = rows // stage_rows
-        if not first_started:
-            tab_copy(tab_h, 0, 0).start()
-
-        def step(i, _):
-            slot = lax.rem(i, 2)
-
-            @pl.when(i + 1 < n)
-            def _():
-                tab_copy(tab_h, i + 1, 1 - slot).start()
-
-            tab_copy(tab_h, i, slot).wait()
-
-            def widen(r, _):
-                at = pl.multiple_of(r * 64, 64)
-                dst = pl.ds(pl.multiple_of(i * stage_rows + at, 64), 64)
-                tab[dst, :] = stage[slot, pl.ds(at, 64), :].astype(jnp.float32)
-                return 0
-
-            lax.fori_loop(0, stage_rows // 64, widen, 0)
+    for n in range(2 * TAB_STEPS):
+        _, tab, step_rows = tabs[n // TAB_STEPS]
+        tab_copy(n).wait()
+
+        def widen(r, _, n=n, tab=tab, step_rows=step_rows):
+            at = pl.multiple_of(r * WIDEN_ROWS, WIDEN_ROWS)
+            dst = pl.ds(pl.multiple_of((n % TAB_STEPS) * step_rows + at, 16), WIDEN_ROWS)
+            tab[dst, :] = stage[n % TAB_SLOTS, pl.ds(at, WIDEN_ROWS), :].astype(jnp.float32)
             return 0
 
-        lax.fori_loop(0, n, step, 0)
-
-    widen_table(tab1_h, tab1, rows_one, True)
-    widen_table(tab2_h, tab2, rows_two, False)
+        lax.fori_loop(0, step_rows // WIDEN_ROWS, widen, 0)
+        if n + TAB_SLOTS < 2 * TAB_STEPS:
+            tab_copy(n + TAB_SLOTS).start()
 
     sub = lax.broadcasted_iota(jnp.int32, (8, LANES), 0)
     lane_id = lax.broadcasted_iota(jnp.int32, (8, LANES), 1)
@@ -220,15 +214,23 @@
 
     lax.fori_loop(0, nchunk, chunk_step, 0)
 
-    def total(r, _):
-        rows = pl.ds(pl.multiple_of(r * 64 + 8, 8), 64)
-        acc[rows, :] = acc[rows, :] + acc2[rows, :]
-        return 0
-
-    lax.fori_loop(0, rows_out // 64, total, 0)
-    cp = pltpu.make_async_copy(acc.at[pl.ds(8, rows_out), :], sum_h, sem_out)
-    cp.start()
-    cp.wait()
+    part = rows_out // OUT_STEPS
+
+    def out_copy(n):
+        src = acc.at[pl.ds(8 + n * part, part), :]
+        return pltpu.make_async_copy(src, sum_h.at[pl.ds(n * part, part), :], sem_out.at[n])
+
+    for n in range(OUT_STEPS):
+
+        def total(r, _, n=n):
+            rows = pl.ds(pl.multiple_of(n * part + r * WIDEN_ROWS + 8, 8), WIDEN_ROWS)
+            acc[rows, :] = acc[rows, :] + acc2[rows, :]
+            return 0
+
+        lax.fori_loop(0, part // WIDEN_ROWS, total, 0)
+        out_copy(n).start()
+    for n in range(OUT_STEPS):
+        out_copy(n).wait()
 
 
 def mttkrp(name, plan, tab1, tab2, rows_out):
@@ -236,14 +238,14 @@
     nnz = line_out.shape[0]
     rows_one, rows_two = tab1.shape[0], tab2.shape[0]
     chunk = min(CHUNK, nnz)
-    stage_rows = 896 if rows_one % 896 == 0 and rows_two % 896 == 0 else 128
+    stage_rows = max(rows_one, rows_two) // TAB_STEPS
     smem = pl.BlockSpec(memory_space=pltpu.SMEM)
     anym = pl.BlockSpec(memory_space=pl.ANY)
     vmem = pl.BlockSpec(memory_space=pltpu.VMEM)
     tiles = (nnz // LANES, LANES)
     step_buf = pltpu.VMEM((8 * UNROLL, LANES), jnp.float32)
     return pl.pallas_call(
-        functools.partial(mttkrp_body, rows_out, rows_one, rows_two, chunk, stage_rows),
+        functools.partial(mttkrp_body, rows_out, rows_one, rows_two, chunk),
         out_shape=jax.ShapeDtypeStruct((rows_out, LANES), jnp.float32),
         in_specs=[smem, smem, anym, anym, anym, vmem, vmem, vmem, anym, anym],
         out_specs=anym,
@@ -252,14 +254,14 @@
             pltpu.VMEM((rows_out + 16, LANES), jnp.float32),
             pltpu.VMEM((rows_one, LANES), jnp.float32),
             pltpu.VMEM((rows_two, LANES), jnp.float32),
-            pltpu.VMEM((2, stage_rows, LANES), jnp.bfloat16),
+            pltpu.VMEM((TAB_SLOTS, stage_rows, LANES), jnp.bfloat16),
             *([step_buf] * 6),
             pltpu.SMEM((2 * chunk,), jnp.int32),
             pltpu.SMEM((2 * chunk,), jnp.int32),
             pltpu.SMEM((2 * chunk,), jnp.int32),
             pltpu.SemaphoreType.DMA((2, 3)),
-            pltpu.SemaphoreType.DMA((2,)),
-            pltpu.SemaphoreType.DMA,
+            pltpu.SemaphoreType.DMA((TAB_SLOTS,)),
+            pltpu.SemaphoreType.DMA((OUT_STEPS,)),
         ],
         name=name,
         compiler_params=pltpu.CompilerParams(vmem_limit_bytes=VMEM_MAX),
@@ -319,8 +321,8 @@
     return ref.at[:, pl.ds(at, w)]
 
 
-def prep_body(b_ref, c_ref, pack_b, pack_c, gram_b, gram_c):
-    for src, pack, gram in ((b_ref, pack_b, gram_b), (c_ref, pack_c, gram_c)):
+def prep_body(b_ref, c_ref, pack_b, pack_c, grams):
+    for src, pack, gram in ((b_ref, pack_b, grams.at[:RANK]), (c_ref, pack_c, grams.at[RANK:])):
         gram[...] = jnp.zeros((RANK, RANK), jnp.float32)
 
         def tile(t, w, src=src, pack=pack, gram=gram):
@@ -333,8 +335,8 @@
 
 def prep(fac_b_t, fac_c_t):
     packs = [jax.ShapeDtypeStruct((lines_of(f.shape[1]), LANES), jnp.bfloat16) for f in (fac_b_t, fac_c_t)]
-    gram = jax.ShapeDtypeStruct((RANK, RANK), jnp.float32)
-    return pl.pallas_call(prep_body, out_shape=(*packs, gram, gram), name="prep")(fac_b_t, fac_c_t)
+    grams = jax.ShapeDtypeStruct((2 * RANK, RANK), jnp.float32)
+    return pl.pallas_call(prep_body, out_shape=(*packs, grams), name="prep")(fac_b_t, fac_c_t)
 
 
 def invert_body(g1_ref, g2_ref, inv_ref, mu_ref, aug):
@@ -428,8 +430,180 @@
     return pl.pallas_call(functools.partial(scale_body, total_rows, want_pack), out_shape=tuple(outs), name=name)(fresh_t, gram_sum)
 
 
-def expand_slab(own_lines, owner_axes):
-    return lax.all_gather(own_lines, owner_axes, axis=0, tiled=True)
+MESH = pl.DeviceIdType.MESH
+
+
+def mate_of(minor, width):
+    return 1 - minor if width == 2 else lax.rem(minor + 2, 4)
+
+
+def twin_of(minor):
+    return minor + 1 - 2 * lax.rem(minor, 2)
+
+
+def meet(peers):
+    barrier = pltpu.get_barrier_semaphore()
+    for peer in peers:
+        pl.semaphore_signal(barrier, inc=1, device_id=peer, device_id_type=MESH)
+    pl.semaphore_wait(barrier, len(peers))
+
+
+class Gather:
+    def __init__(self, line_axis, n_line, minor_axis, width, own, out, sems):
+        self.line_axis, self.n_line, self.minor_axis, self.width = line_axis, n_line, minor_axis, width
+        self.own, self.out = own, out
+        self.line, self.minor = lax.axis_index(line_axis), lax.axis_index(minor_axis)
+        self.local, self.sl, self.rl, self.sp, self.rp, self.sc, self.rc = sems
+        self.lines = own.shape[0]
+        self.part = self.lines // GATHER_PARTS
+        self.cores = width == 4
+        self.mate = {minor_axis: mate_of(self.minor, width)}
+        self.twin = {minor_axis: twin_of(self.minor)}
+        self.others = [lax.rem(self.line + d, n_line) for d in range(1, n_line)]
+        self.started = []
+
+    def peers(self):
+        return [{self.line_axis: l} for l in self.others] + [self.mate] + ([self.twin] if self.cores else [])
+
+    def rows(self, line, minor, k):
+        return self.out.at[pl.ds((line * self.width + minor) * self.lines + k * self.part, self.part), :]
+
+    def send(self, src, dst, send_sem, recv_sem, peer):
+        cp = pltpu.make_async_remote_copy(src, dst, send_sem, recv_sem, device_id=peer, device_id_type=MESH)
+        cp.start()
+        self.started.append(cp)
+
+    def expect(self, dst, recv_sem, send_sem):
+        pltpu.make_async_remote_copy(dst, dst, send_sem, recv_sem, device_id=self.mate, device_id_type=MESH).wait_recv()
+
+    def to_mate(self, src, line, k):
+        self.send(src, self.rows(line, self.minor, k), self.sp.at[line, k], self.rp.at[line, k], self.mate)
+
+    def to_twin(self, src, line, minor, side, k):
+        if self.cores:
+            self.send(src, self.rows(line, minor, k), self.sc.at[line, side, k], self.rc.at[line, side, k], self.twin)
+
+    def begin(self):
+        for k in range(GATHER_PARTS):
+            src = self.own.at[pl.ds(k * self.part, self.part), :]
+            self.to_mate(src, self.line, k)
+            for l in self.others:
+                self.send(src, self.rows(self.line, self.minor, k), self.sl.at[l, k], self.rl.at[self.line, k], {self.line_axis: l})
+            self.to_twin(src, self.line, self.minor, 0, k)
+        self.keep = pltpu.make_async_copy(self.own, self.out.at[pl.ds((self.line * self.width + self.minor) * self.lines, self.lines), :], self.local)
+        self.keep.start()
+
+    def from_line(self, line):
+        for k in range(GATHER_PARTS):
+            rows = self.rows(line, self.minor, k)
+            self.expect(rows, self.rl.at[line, k], self.sl.at[line, k])
+            self.to_mate(rows, line, k)
+            self.to_twin(rows, line, self.minor, 0, k)
+
+    def from_mate(self, line):
+        minor = mate_of(self.minor, self.width)
+        for k in range(GATHER_PARTS):
+            rows = self.rows(line, minor, k)
+            self.expect(rows, self.rp.at[line, k], self.sp.at[line, k])
+            self.to_twin(rows, line, minor, 1, k)
+
+    def middle(self):
+        order = [lax.rem(self.line + d, self.n_line) for d in range(self.n_line - 1, 0, -1)]
+        previous = self.line
+        for line in order:
+            self.from_line(line)
+            self.from_mate(previous)
+            previous = line
+        self.from_mate(previous)
+
+    def end(self):
+        if self.cores:
+            twin = twin_of(self.minor)
+            for line in [self.line, *self.others]:
+                for side, minor in enumerate((twin, mate_of(twin, self.width))):
+                    for k in range(GATHER_PARTS):
+                        self.expect(self.rows(line, minor, k), self.rc.at[line, side, k], self.sc.at[line, side, k])
+        for cp in self.started:
+            cp.wait_send()
+        self.keep.wait()
+
+
+def gather_body(specs, *refs):
+    n = len(specs)
+    owns, outs, sems = refs[:n], refs[n : 2 * n], refs[2 * n :]
+    gathers = [Gather(*spec, own, out, sems[7 * i : 7 * i + 7]) for i, (spec, own, out) in enumerate(zip(specs, owns, outs))]
+    meet([peer for g in gathers for peer in g.peers()])
+    for g in gathers:
+        g.begin()
+    for g in gathers:
+        g.middle()
+    for g in gathers:
+        g.end()
+
+
+def expand_slabs(name, collective_id, specs, owns):
+    dma = pltpu.SemaphoreType.DMA
+    scratch = []
+    for _, n_line, _, _ in specs:
+        flat, sided = dma((n_line, GATHER_PARTS)), dma((n_line, 2, GATHER_PARTS))
+        scratch += [dma, flat, flat, flat, flat, sided, sided]
+    outs = [jax.ShapeDtypeStruct((s[1] * s[3] * o.shape[0], LANES), o.dtype) for s, o in zip(specs, owns)]
+    return pl.pallas_call(
+        functools.partial(gather_body, specs),
+        out_shape=tuple(outs),
+        in_specs=[pl.BlockSpec(memory_space=pltpu.VMEM)] * len(owns),
+        out_specs=tuple([pl.BlockSpec(memory_space=pl.ANY)] * len(owns)),
+        scratch_shapes=scratch,
+        name=name,
+        compiler_params=pltpu.CompilerParams(collective_id=collective_id, has_side_effects=True),
+    )(*owns)
+
+
+def sum_body(sizes, x_ref, out_ref, cur, *rest):
+    n = len(sizes)
+    slots, sends, recvs = rest[:n], rest[n : 2 * n], rest[2 * n :]
+    me = [lax.axis_index(axis) for axis, _ in sizes]
+    others = [[lax.rem(m + d, size) for d in range(1, size)] for m, (_, size) in zip(me, sizes)]
+    meet([{axis: o} for (axis, _), os in zip(sizes, others) for o in os])
+    src = x_ref
+    for i, (axis, size) in enumerate(sizes):
+        copies = []
+        for o in others[i]:
+            cp = pltpu.make_async_remote_copy(
+                src, slots[i].at[me[i]], sends[i].at[o], recvs[i].at[me[i]], device_id={axis: o}, device_id_type=MESH
+            )
+            cp.start()
+            copies.append(cp)
+        slots[i][me[i]] = src[...]
+        for o in others[i]:
+            pltpu.make_async_remote_copy(
+                src, slots[i].at[o], sends[i].at[o], recvs[i].at[o], device_id={axis: o}, device_id_type=MESH
+            ).wait_recv()
+        total = slots[i][0]
+        for k in range(1, size):
+            total = total + slots[i][k]
+        for cp in copies:
+            cp.wait_send()
+        dst = out_ref if i == n - 1 else cur.at[i]
+        dst[...] = total
+        src = dst
+
+
+def sum_all(name, collective_id, mesh_sizes, x):
+    n = len(mesh_sizes)
+    dma = pltpu.SemaphoreType.DMA
+    scratch = [pltpu.VMEM((n - 1, *x.shape), x.dtype)]
+    scratch += [pltpu.VMEM((size, *x.shape), x.dtype) for _, size in mesh_sizes]
+    scratch += [dma((size,)) for _, size in mesh_sizes] * 2
+    return pl.pallas_call(
+        functools.partial(sum_body, mesh_sizes),
+        out_shape=jax.ShapeDtypeStruct(x.shape, x.dtype),
+        in_specs=[pl.BlockSpec(memory_space=pltpu.VMEM)],
+        out_specs=pl.BlockSpec(memory_space=pltpu.VMEM),
+        scratch_shapes=scratch,
+        name=name,
+        compiler_params=pltpu.CompilerParams(collective_id=collective_id, has_side_effects=True),
+    )(x)
 
 
 def fold_slab(part_lines, owner_axes):
@@ -452,10 +626,14 @@
         rows_c = lines_of(own_c) * (n_dev // size_z)
         old_a, old_b, old_c = fac_a.T, fac_b.T, fac_c.T
 
-        pack_b, pack_c, gram_b, gram_c = prep(old_b, old_c)
-        gram_b, gram_c = lax.psum((gram_b, gram_c), ALL_AXES)
-        buf_b = expand_slab(pack_b, owners_b)
-        buf_c = expand_slab(pack_c, owners_c)
+        sizes = (("gx", size_x), ("gz", size_z), ("gy", size_y))
+        spec_a = ("gz", size_z, "gy", size_y)
+        spec_b = ("gz", size_z, "gx", size_x)
+        spec_c = ("gy", size_y, "gx", size_x)
+        pack_b, pack_c, grams = prep(old_b, old_c)
+        buf_c, buf_b = expand_slabs("gather_bc", 0, (spec_c, spec_b), (pack_c, pack_b))
+        grams = sum_all("sum_bc", 1, sizes, grams)
+        gram_b, gram_c = grams[:RANK], grams[RANK:]
 
         at_a = place_rows(idx_i, own_a)
         at_b = place_rows(idx_j, own_b)
@@ -467,31 +645,31 @@
         part_a = mttkrp("mttkrp_a", plan_a, buf_b, buf_c, rows_a)
         inv, mu = invert("invert_a", gram_b, gram_c)
         fresh, gram = solve("solve_a", fold_slab(part_a, owners_a), old_a, inv, mu)
-        out_a, _, gram_a, pack_a = scale("scale_a", fresh, lax.psum(gram, ALL_AXES), own_a * n_dev, True)
-        buf_a = expand_slab(pack_a, owners_a)
+        out_a, _, gram_a, pack_a = scale("scale_a", fresh, sum_all("sum_a", 2, sizes, gram), own_a * n_dev, True)
+        (buf_a,) = expand_slabs("gather_a", 3, (spec_a,), (pack_a,))
 
         plan_b = plan_mode(nblk, nz_vals, at_b, at_a, at_c, rows_b)
         part_b = mttkrp("mttkrp_b", plan_b, buf_a, buf_c, rows_b)
         inv, mu = invert("invert_b", gram_a, gram_c)
         fresh, gram = solve("solve_b", fold_slab(part_b, owners_b), old_b, inv, mu)
-        out_b, _, gram_nb, pack_nb = scale("scale_b", fresh, lax.psum(gram, ALL_AXES), own_b * n_dev, True)
-        buf_nb = expand_slab(pack_nb, owners_b)
+        out_b, _, gram_nb, pack_nb = scale("scale_b", fresh, sum_all("sum_b", 4, sizes, gram), own_b * n_dev, True)
+        (buf_nb,) = expand_slabs("gather_b", 5, (spec_b,), (pack_nb,))
 
         plan_c = plan_mode(nblk, nz_vals, at_c, at_a, at_b, rows_c)
         part_c = mttkrp("mttkrp_c", plan_c, buf_a, buf_nb, rows_c)
         inv, mu = invert("invert_c", gram_a, gram_nb)
         fresh, gram = solve("solve_c", fold_slab(part_c, owners_c), old_c, inv, mu)
-        out_c, lambdas, _ = scale("scale_c", fresh, lax.psum(gram, ALL_AXES), own_c * n_dev, False)
+        out_c, lambdas, _ = scale("scale_c", fresh, sum_all("sum_c", 6, sizes, gram), own_c * n_dev, False)
         return out_a.T, out_b.T, out_c.T, lambdas.reshape(RANK)
 
-    spec_nz = P(("gz", "gy", "gx"))
-    spec_a = P(("gx", "gz", "gy"), None)
-    spec_b = P(("gy", "gz", "gx"), None)
-    spec_c = P(("gz", "gy", "gx"), None)
+    part_nz = P(("gz", "gy", "gx"))
+    part_a = P(("gx", "gz", "gy"), None)
+    part_b = P(("gy", "gz", "gx"), None)
+    part_c = P(("gz", "gy", "gx"), None)
     return jax.shard_map(
         device_step,
         mesh=mesh,
-        in_specs=(spec_nz, spec_nz, spec_nz, spec_nz, spec_a, spec_b, spec_c),
-        out_specs=(spec_a, spec_b, spec_c, P()),
+        in_specs=(part_nz, part_nz, part_nz, part_nz, part_a, part_b, part_c),
+        out_specs=(part_a, part_b, part_c, P()),
         check_vma=False,
     )

time: 1940 us -> 1480 us (0.76); the launches traced: 1910 us -> 1480 us
  waiting for transfers between devices: 752 us -> 507 us
  blocking collectives: 161 us -> 0 us
  Pallas kernels: 961 us -> 933 us
    pallas_call x3, Pallas kernels: 874 us -> 522 us  [mttkrp(): pl.pallas_call(functools.partial(mttkrp_body, rows_out, rows_one, rows_tw...]
    pallas_call x1 -> x8, Pallas kernels: 7.92 us -> 332 us  [the longest x3 259 us: expand_slabs(): pl.pallas_call(functools.partial(gather_body, specs), out_shape=tuple(out...]
    all_gather x4 -> x0, waiting for transfers between devices: 295 us -> none  [expand_slab(): return lax.all_gather(own_lines, owner_axes, axis=0, tiled=True)]
    psum x4 -> x0, blocking collectives: 161 us -> none  [the longest x3 121 us: device_step(): lax.psum(gram, ALL_AXES)]
    reduce_scatter x3, waiting for transfers between devices: 456 us -> 507 us  [fold_slab(): lax.psum_scatter(part_lines, owner_axes, scatter_dimension=0, tiled=True)]
  transfers between devices with their start and end apart: 7 -> 3, of which waited for: 7 -> 3; matrix products, arithmetic and copies ran while one was open for 1% -> 0% of each run, Pallas kernels for 1% -> 3%
where the time goes in v2:
time: 1480 us
  Pallas kernels  933 us (63%)
  waiting for transfers between devices  507 us (34%)
    pallas_call x3, Pallas kernels, mttkrp(): pl.pallas_call(functools.partial(mttkrp_body, rows_out, rows_one, rows_tw...  522 us
    reduce_scatter x3, waiting for transfers between devices, fold_slab(): lax.psum_scatter(part_lines, owner_axes, scatter_dimension=0, tiled=True)  507 us
    pallas_call x3, Pallas kernels, expand_slabs(): pl.pallas_call(functools.partial(gather_body, specs), out_shape=tuple(out...  259 us
    pallas_call x4, Pallas kernels, sum_all(): pl.pallas_call(functools.partial(sum_body, mesh_sizes), out_shape=jax.Sha...  65.3 us
    pallas_call x3, Pallas kernels, solve(): pl.pallas_call(solve_body, out_shape=(jax.ShapeDtypeStruct(old_t.shape, j...  43.4 us
  transfers between devices with their start and end apart: 3, of which 3 were waited for; matrix products, arithmetic and copies ran while one was open for 0% of the time, Pallas kernels for 3%

profile of v2, /device:TPU:0, one launch (start us, length us, event | category | flops | bytes accessed | tf_op | source)
XLA Modules:
  0.0 1476.5 jit_solution(6423210399875151809)
XLA Ops:
  7.3 1.4 convolution_convert_fusion.4
  8.6 1.6 convolution_convert_fusion.5
  10.3 1.3 convolution_convert_fusion.3
  11.6 1.3 convolution_convert_fusion.2
  13.0 0.6 fusion
  13.7 1.0 bitcast_subtract_fusion
  14.7 1.4 bitcast_subtract_fusion.1
  16.1 0.7 copy-done.3
  16.8 1.8 bitcast_subtract_fusion.3
  19.2 0.1 fusion.59
  19.4 0.1 fusion.19
  19.5 0.1 fusion.20
  19.6 0.1 fusion.60
  20.8 0.2 convolution_convert_fusion.8
  21.1 0.7 reshape.132.flag_ref
  21.8 0.6 fusion.128
  22.4 7.9 prep.1
  30.2 69.6 %gather_bc.1 = (bf16[14336,128]{1,0:T(8,128)(2,1)}, bf16[28672,128]{1,0:T(8,128)(2,1)}) custom-call(bf16[1792,128]{1,0:T(8,128)(2,1)} %get-tuple-element.29.refs_0_, bf16[1792,128]{1,0:T(8,128)(2,1)} %get-tuple-element.30.refs_1_), custom_call_target="tpu_custom_call" | custom-call | tf_op jit(solution)/shard_map/gather_bc/pallas_call | solution.py:551
  99.9 1.1 add_add_fusion.2
  101.0 173.6 %mttkrp_a.1 = f32[37888,128]{1,0:T(8,128)} custom-call(s32[1]{0:T(128)} %bitcast.nblk_ref, s32[512]{0:T(512)} %reshape.132.flag_ref, s32[65536]{0:T(1024)} %get-tuple-element.75.out_h, s32[65536]{0:T(1024)} %copy-done.3, s32[65536]{0:T(1024)} %copy-done.5, f32[512,128]{1,0:T(8,128)} %bitcast.54, s32[512,128]{1,0:T(8,128)} %get-tuple-element.81.code_ref, ...), custom_call_target="tpu_custom_call" | custom-call | flops 2000000000 | bytes 50000000 | tf_op jit(solution)/shard_map/mttkrp_a/pallas_call | solution.py:247
  274.7 21.7 %sum_bc.1 = f32[128,64]{1,0:T(8,128)} custom-call(f32[128,64]{1,0:T(8,128)} %get-tuple-element.33.x_ref), custom_call_target="tpu_custom_call" | custom-call | tf_op jit(solution)/shard_map/sum_bc/pallas_call | solution.py:598
  297.1 0.1 and_reduce_fusion.1
  297.4 0.2 convolution_convert_fusion.7
  297.7 0.6 reshape.135.flag_ref
  298.3 1.4 fusion.129
  299.7 7.6 invert_a.1
  307.4 286.8 %reduce-scatter.4.cloned.1.call-done.m_ref = f32[4736,128]{1,0:T(8,128)} async-done(((f32[37888,128]{1,0:T(8,128)}), f32[4736,128]{1,0:T(8,128)}) %reduce-scatter.4.cloned.1.call-update) | async-done | bytes 2424848 | tf_op jit(solution)/shard_map/reduce_scatter | solution.py:610
  594.2 23.9 %solve_a.1 = (f32[64,9408]{1,0:T(8,128)}, f32[64,64]{1,0:T(8,128)}) custom-call(f32[4736,128]{1,0:T(8,128)} %reduce-scatter.4.cloned.1.call-done.m_ref, f32[64,9408]{1,0:T(8,128)} %bitcast.61, f32[64,64]{1,0:T(8,128)} %get-tuple-element.34.inv_ref, f32[8,128]{1,0:T(8,128)} %get-tuple-element.35.mu_ref), custom_call_target="tpu_custom_call" | custom-call | tf_op jit(solution)/shard_map/solve_a/pallas_call | solution.py:395
  618.1 14.5 sum_a.1.gram_ref
  632.6 7.3 scale_a.1
  639.9 134.5 %gather_a.1.tab1_h = bf16[37888,128]{1,0:T(8,128)(2,1)} custom-call(bf16[4736,128]{1,0:T(8,128)(2,1)} %get-tuple-element.39.refs_0_), custom_call_target="tpu_custom_call" | custom-call | tf_op jit(solution)/shard_map/gather_a/pallas_call | solution.py:551
  774.4 173.2 %mttkrp_b.1 = f32[28672,128]{1,0:T(8,128)} custom-call(s32[1]{0:T(128)} %bitcast.nblk_ref, s32[512]{0:T(512)} %reshape.135.flag_ref, s32[65536]{0:T(1024)} %get-tuple-element.73.out_h, s32[65536]{0:T(1024)} %copy-done.4, s32[65536]{0:T(1024)} %copy-done.5, f32[512,128]{1,0:T(8,128)} %bitcast.55, s32[512,128]{1,0:T(8,128)} %get-tuple-element.80.code_ref, ...), custom_call_target="tpu_custom_call" | custom-call | flops 2000000000 | bytes 50000000 | tf_op jit(solution)/shard_map/mttkrp_b/pallas_call | solution.py:247
  947.6 0.2 reduce-scatter.8.cloned.1.call-start
  947.9 0.7 copy-done
  949.4 0.2 convolution_convert_fusion.6
  949.8 0.7 reshape.137.flag_ref
  950.5 7.6 invert_b.1
  958.1 155.6 %reduce-scatter.6.cloned.1.call-done.m_ref = f32[1792,128]{1,0:T(8,128)} async-done(((f32[28672,128]{1,0:T(8,128)}), f32[1792,128]{1,0:T(8,128)}) %reduce-scatter.6.cloned.1.call-update) | async-done | bytes 917520 | tf_op jit(solution)/shard_map/reduce_scatter | solution.py:610
  1113.7 9.7 solve_b.1
  1123.4 14.5 sum_b.1.gram_ref
  1137.9 3.6 scale_b.1
  1141.4 55.0 %gather_b.1.tab2_h = bf16[28672,128]{1,0:T(8,128)(2,1)} custom-call(bf16[1792,128]{1,0:T(8,128)(2,1)} %get-tuple-element.46.refs_0_), custom_call_target="tpu_custom_call" | custom-call | tf_op jit(solution)/shard_map/gather_b/pallas_call | solution.py:551
  1196.5 174.8 %mttkrp_c.1 = f32[14336,128]{1,0:T(8,128)} custom-call(s32[1]{0:T(128)} %bitcast.nblk_ref, s32[512]{0:T(512)} %reshape.137.flag_ref, s32[65536]{0:T(1024)} %get-tuple-element.61.out_h, s32[65536]{0:T(1024)} %copy-done.4, s32[65536]{0:T(1024)} %copy-done.3, f32[512,128]{1,0:T(8,128)} %bitcast.56, s32[512,128]{1,0:T(8,128)} %get-tuple-element.79.code_ref, ...), custom_call_target="tpu_custom_call" | custom-call | flops 2000000000 | bytes 50000000 | tf_op jit(solution)/shard_map/mttkrp_c/pallas_call | solution.py:247
  1371.3 7.6 invert_c.1
  1379.0 64.2 %reduce-scatter.8.cloned.1.call-done.m_ref = f32[1792,128]{1,0:T(8,128)} async-done(((f32[14336,128]{1,0:T(8,128)}), f32[1792,128]{1,0:T(8,128)}) %reduce-scatter.8.cloned.1.call-update) | async-done | bytes 917520 | tf_op jit(solution)/shard_map/reduce_scatter | solution.py:610
  1443.2 9.8 solve_c.1
  1453.0 14.6 sum_c.1.gram_ref
  1467.6 2.3 scale_c.1
  (49 shorter events, 3.1 us)
Async XLA Ops:
  7.2 7.6 copy-start.8
  7.2 5.8 copy-start.6
  7.2 5.8 copy-start.7
  7.2 6.5 copy-start.2
  7.2 587.0 %reduce-scatter.4.cloned.1.call-start = ((), (), s32[]{:S(2)}) async-start(), calls=%async_computation.3 | async-start | bytes 21823488 | tf_op jit(solution)/shard_map/reduce_scatter | solution.py:610
  14.7 3.8 copy-start.5
  16.1 0.7 copy-start.3
  16.1 2.5 copy-start.4
  274.6 21.8 %copy-start.1 = (s32[64,8,128]{2,1,0:T(8,128)S(1)}, s32[64,8,128]{2,1,0:T(8,128)}, u32[]{:S(2)}) copy-start(s32[64,8,128]{2,1,0:T(8,128)} %get-tuple-element.72) | copy-start | bytes 786436
  274.7 839.0 %reduce-scatter.6.cloned.1.call-start = ((), (), s32[]{:S(2)}) async-start(), calls=%async_computation.4 | async-start | bytes 15597568 | tf_op jit(solution)/shard_map/reduce_scatter | solution.py:610
  947.6 1.0 copy-start
  947.6 495.5 %reduce-scatter.8.cloned.1.call-start = ((), (), s32[]{:S(2)}) async-start(), calls=%async_computation.5 | async-start | bytes 8257536 | tf_op jit(solution)/shard_map/reduce_scatter | solution.py:610
Sparse Core Ops, SparseCore 0:
  274.8 319.3 reduce-scatter.3
  947.8 165.8 reduce-scatter.5
  1371.4 71.6 reduce-scatter.7

commit v3 on v2

--- a/solution.py
+++ b/solution.py
@@ -1,4 +1,6 @@
 import functools
+import itertools
+import math
 
 import jax
 import jax.numpy as jnp
@@ -21,7 +23,8 @@
 TAB_SLOTS = 3
 OUT_STEPS = 8
 WIDEN_ROWS = 32
-GATHER_PARTS = 2
+GATHER_PARTS = 4
+FOLD_LAG = 2
 
 
 def lines_of(own_rows):
@@ -606,8 +609,170 @@
     )(x)
 
 
-def fold_slab(part_lines, owner_axes):
-    return lax.psum_scatter(part_lines, owner_axes, scatter_dimension=0, tiled=True)
+class Fold:
+    def __init__(self, dims, colors, pieces, x, own, out, bufs, sends, recvs, local):
+        self.dims, self.colors, self.pieces = dims, colors, pieces
+        self.names = [name for name, _ in dims]
+        self.size = dict(dims)
+        self.x, self.own, self.out, self.local = x, own, out, local
+        gx = lax.axis_index("gx")
+        self.at = {"z": lax.axis_index("gz"), "y": lax.axis_index("gy"), "x": lax.div(gx, 2), "c": lax.rem(gx, 2)}
+        self.flows = []
+        first_line, n = 0, 0
+        for order, lines in colors:
+            off = 0
+            for j, name in enumerate(order):
+                lag = 1 if name == "c" else FOLD_LAG
+                for way in (1, -1):
+                    self.flows.append((order, j, lines, first_line, off, lag, way, bufs[n], sends.at[n], recvs.at[n]))
+                    n += 1
+                off += lag * (self.size[name] - 1)
+            first_line += lines * pieces
+            self.last = off
+
+    def peer(self, name, pos):
+        if name == "z":
+            return {"gz": pos}
+        if name == "y":
+            return {"gy": pos}
+        return {"gx": pos * 2 + self.at["c"] if name == "x" else self.at["x"] * 2 + pos}
+
+    def peers(self):
+        found = []
+        for name, size in self.dims:
+            found += [self.peer(name, lax.rem(self.at[name] + d, size)) for d in range(1, size)]
+        return found
+
+    def view(self, ref, order, j, current, lines):
+        index = [self.at[d] if d in order[:j] else current if d == order[j] else slice(None) for d in self.names]
+        return ref.at[(*index, lines, slice(None))]
+
+    def slot(self, buf, order, j, current, lines):
+        left = [d for d in self.names if d not in order[:j]]
+        return buf.at[(*[current if d == order[j] else slice(None) for d in left], lines, slice(None))]
+
+    def rows(self, flow, c):
+        _, _, lines, first, *_ = flow
+        return pl.ds(pl.multiple_of(first + c * lines, 8), lines), pl.ds(pl.multiple_of(c * lines, 8), lines)
+
+    def copy(self, flow, p, c):
+        order, j, _, _, _, _, way, buf, send, recv = flow
+        n = self.size[order[j]]
+        count = n - 1 - p if way > 0 else p
+        mine, theirs = self.rows(flow, c)
+        blocks = slice(p + 1, n) if way > 0 else slice(0, p)
+        src = self.view(self.x if j == 0 and count == n - 1 else self.own, order, j, blocks, mine)
+        dst = self.slot(buf, order, j, slice(0, count), theirs)
+        return pltpu.make_async_remote_copy(
+            src, dst, send.at[c], recv.at[c], device_id=self.peer(order[j], p + way), device_id_type=MESH
+        )
+
+    def take(self, flow, p, c):
+        order, j, _, _, _, _, way, buf, send, recv = flow
+        n = self.size[order[j]]
+        count = n - p if way > 0 else p + 1
+        first = p if way > 0 else 0
+        mine, theirs = self.rows(flow, c)
+        dst = self.slot(buf, order, j, slice(0, count), theirs)
+        pltpu.make_async_remote_copy(
+            dst, dst, send.at[c], recv.at[c], device_id=self.peer(order[j], p - way), device_id_type=MESH
+        ).wait_recv()
+        left = [d for d in self.names if d not in order[:j]]
+        for place in itertools.product(*[range(count if d == order[j] else self.size[d]) for d in left]):
+            spot = dict(zip(left, place))
+            at = [self.at[d] if d in order[:j] else spot[d] + (first if d == order[j] else 0) for d in self.names]
+            at = (*at, mine, slice(None))
+            self.own[at] = self.own[at] + buf[(*place, theirs, slice(None))]
+
+    def each(self, s, act, wants):
+        for flow in self.flows:
+            order, j, _, _, off, lag, way = flow[:7]
+            n = self.size[order[j]]
+            for p in range(n):
+                hop = p if way > 0 else n - 1 - p
+                if not wants(hop, n):
+                    continue
+                c = s - off - lag * hop
+
+                @pl.when((self.at[order[j]] == p) & (c >= 0) & (c < self.pieces))
+                def _(flow=flow, p=p, c=c):
+                    act(flow, p, c)
+
+    def run(self):
+        load = pltpu.make_async_copy(self.x, self.own, self.local)
+        load.start()
+        steps = self.pieces + self.last
+        sends = lambda hop, n: hop < n - 1
+        takes = lambda hop, n: hop > 0
+
+        def step(s, _):
+            @pl.when(s == 1)
+            def _():
+                load.wait()
+
+            self.each(s, self.take, takes)
+            self.each(s, lambda f, p, c: self.copy(f, p, c).start(), sends)
+            return 0
+
+        lax.fori_loop(0, steps, step, 0)
+        index = tuple(self.at[d] for d in self.names)
+        keep = pltpu.make_async_copy(self.own.at[index], self.out, self.local)
+        keep.start()
+
+        def drain(s, _):
+            self.each(s, lambda f, p, c: self.copy(f, p, c).wait_send(), sends)
+            return 0
+
+        lax.fori_loop(0, steps, drain, 0)
+        keep.wait()
+
+
+def fold_body(dims, colors, pieces, n_flows, x, out, own, *rest):
+    bufs, (sends, recvs, local) = rest[:n_flows], rest[n_flows:]
+    fold = Fold(dims, colors, pieces, x, own, out, bufs, sends, recvs, local)
+    meet(fold.peers())
+    fold.run()
+
+
+def fold_plan(kind, lines):
+    if kind == "a":
+        dims, orders, share = (("z", 4), ("y", 2)), (("y", "z"), ("z", "y")), (56, 8)
+    elif kind == "b":
+        dims, orders, share = (("z", 4), ("x", 2), ("c", 2)), (("c", "x", "z"), ("c", "z", "x")), (24, 8)
+    else:
+        dims, orders, share = (("y", 2), ("x", 2), ("c", 2)), (("c", "x", "y"), ("c", "y", "x")), (32, 32)
+    return dims, tuple(zip(orders, share)), lines // sum(share)
+
+
+def fold_slab(name, collective_id, kind, part_lines):
+    dims, _, _ = fold_plan(kind, 0)
+    grid = tuple(size for _, size in dims)
+    lines = part_lines.shape[0] // math.prod(grid)
+    dims, colors, pieces = fold_plan(kind, lines)
+    size = dict(dims)
+    bufs = []
+    for order, share in colors:
+        for j, axis in enumerate(order):
+            left = [size[d] - (d == axis) for d, _ in dims if d not in order[:j]]
+            bufs += [pltpu.VMEM((*left, share * pieces, LANES), jnp.float32)] * 2
+    dma = pltpu.SemaphoreType.DMA
+    return pl.pallas_call(
+        functools.partial(fold_body, dims, colors, pieces, len(bufs)),
+        out_shape=jax.ShapeDtypeStruct((lines, LANES), jnp.float32),
+        in_specs=[pl.BlockSpec(memory_space=pl.ANY)],
+        out_specs=pl.BlockSpec(memory_space=pl.ANY),
+        scratch_shapes=[
+            pltpu.VMEM((*grid, lines, LANES), jnp.float32),
+            *bufs,
+            dma((len(bufs), pieces)),
+            dma((len(bufs), pieces)),
+            dma,
+        ],
+        name=name,
+        compiler_params=pltpu.CompilerParams(
+            collective_id=collective_id, has_side_effects=True, vmem_limit_bytes=VMEM_MAX
+        ),
+    )(part_lines.reshape(*grid, lines, LANES))
 
 
 def solution(mesh):
@@ -615,9 +780,6 @@
     size_y = mesh.shape["gy"]
     size_x = mesh.shape["gx"]
     n_dev = size_z * size_y * size_x
-    owners_a = ("gz", "gy")
-    owners_b = ("gz", "gx")
-    owners_c = ("gy", "gx")
 
     def device_step(nz_vals, idx_i, idx_j, idx_k, fac_a, fac_b, fac_c):
         own_a, own_b, own_c = fac_a.shape[0], fac_b.shape[0], fac_c.shape[0]
@@ -644,21 +806,21 @@
         plan_a = plan_mode(nblk, nz_vals, at_a, at_b, at_c, rows_a)
         part_a = mttkrp("mttkrp_a", plan_a, buf_b, buf_c, rows_a)
         inv, mu = invert("invert_a", gram_b, gram_c)
-        fresh, gram = solve("solve_a", fold_slab(part_a, owners_a), old_a, inv, mu)
+        fresh, gram = solve("solve_a", fold_slab("fold_a", 7, "a", part_a), old_a, inv, mu)
         out_a, _, gram_a, pack_a = scale("scale_a", fresh, sum_all("sum_a", 2, sizes, gram), own_a * n_dev, True)
         (buf_a,) = expand_slabs("gather_a", 3, (spec_a,), (pack_a,))
 
         plan_b = plan_mode(nblk, nz_vals, at_b, at_a, at_c, rows_b)
         part_b = mttkrp("mttkrp_b", plan_b, buf_a, buf_c, rows_b)
         inv, mu = invert("invert_b", gram_a, gram_c)
-        fresh, gram = solve("solve_b", fold_slab(part_b, owners_b), old_b, inv, mu)
+        fresh, gram = solve("solve_b", fold_slab("fold_b", 8, "b", part_b), old_b, inv, mu)
         out_b, _, gram_nb, pack_nb = scale("scale_b", fresh, sum_all("sum_b", 4, sizes, gram), own_b * n_dev, True)
         (buf_nb,) = expand_slabs("gather_b", 5, (spec_b,), (pack_nb,))
 
         plan_c = plan_mode(nblk, nz_vals, at_c, at_a, at_b, rows_c)
         part_c = mttkrp("mttkrp_c", plan_c, buf_a, buf_nb, rows_c)
         inv, mu = invert("invert_c", gram_a, gram_nb)
-        fresh, gram = solve("solve_c", fold_slab(part_c, owners_c), old_c, inv, mu)
+        fresh, gram = solve("solve_c", fold_slab("fold_c", 9, "c", part_c), old_c, inv, mu)
         out_c, lambdas, _ = scale("scale_c", fresh, sum_all("sum_c", 6, sizes, gram), own_c * n_dev, False)
         return out_a.T, out_b.T, out_c.T, lambdas.reshape(RANK)
 

time: 1480 us -> 1360 us (0.919)
  waiting for transfers between devices: 507 us -> 0 us
  Pallas kernels: 933 us -> 1330 us
    reduce_scatter x3 -> x0, waiting for transfers between devices: 507 us -> none  [fold_slab(): lax.psum_scatter(part_lines, owner_axes, scatter_dimension=0, tiled=True)]
    pallas_call x0 -> x3, Pallas kernels: none -> 404 us  [fold_slab(): pl.pallas_call(functools.partial(fold_body, dims, colors, pieces, len(buf...]
  transfers between devices with their start and end apart: 3 -> 0, of which waited for: 3 -> 0; matrix products, arithmetic and copies ran while one was open for 0% -> 0% of each run, Pallas kernels for 3% -> 0%
where the time goes in v3:
time: 1360 us; the launch traced here: 1350 us
  Pallas kernels  1330 us (98%)
    pallas_call x3, Pallas kernels, mttkrp(): pl.pallas_call(functools.partial(mttkrp_body, rows_out, rows_one, rows_tw...  522 us
    pallas_call x3, Pallas kernels, fold_slab(): pl.pallas_call(functools.partial(fold_body, dims, colors, pieces, len(buf...  404 us
    pallas_call x3, Pallas kernels, expand_slabs(): pl.pallas_call(functools.partial(gather_body, specs), out_shape=tuple(out...  259 us
    pallas_call x4, Pallas kernels, sum_all(): pl.pallas_call(functools.partial(sum_body, mesh_sizes), out_shape=jax.Sha...  60.1 us
    pallas_call x3, Pallas kernels, solve(): pl.pallas_call(solve_body, out_shape=(jax.ShapeDtypeStruct(old_t.shape, j...  43.4 us

profile of v3, /device:TPU:0, one launch (start us, length us, event | category | flops | bytes accessed | tf_op | source)
XLA Modules:
  0.0 1354.9 jit_solution(2377077461978541441)
XLA Ops:
  0.8 1.7 convolution_convert_fusion.5
  2.4 1.3 convolution_convert_fusion.4
  3.8 1.4 convolution_convert_fusion.3
  5.1 1.3 convolution_convert_fusion.2
  7.1 0.6 fusion
  7.8 0.6 fusion.128
  8.4 1.2 add_add_fusion.2
  9.5 1.0 bitcast_subtract_fusion
  10.6 8.0 prep.1
  18.5 20.9 %sum_bc.1 = f32[128,64]{1,0:T(8,128)} custom-call(f32[128,64]{1,0:T(8,128)} %get-tuple-element.33.x_ref), custom_call_target="tpu_custom_call" | custom-call | tf_op jit(solution)/shard_map/sum_bc/pallas_call | solution.py:601
  39.4 1.4 fusion.129
  40.8 7.6 invert_a.1
  48.4 1.4 bitcast_subtract_fusion.1
  49.8 0.7 copy-done.1
  50.5 1.6 bitcast_subtract_fusion.3
  53.6 0.2 convolution_convert_fusion.8
  53.9 0.3 fusion.55
  54.2 0.3 fusion.13
  54.4 0.3 fusion.14
  54.7 0.3 fusion.56
  55.0 0.3 fusion.15
  55.2 0.3 and_reduce_fusion
  55.5 0.1 compare_and_fusion
  55.7 0.2 convolution_convert_fusion.7
  55.9 0.3 convolution_convert_fusion.6
  56.3 0.7 reshape.148.flag_ref
  57.0 0.7 reshape.145.flag_ref
  57.8 0.7 reshape.141.flag_ref
  58.5 67.7 %gather_bc.1 = (bf16[14336,128]{1,0:T(8,128)(2,1)}, bf16[28672,128]{1,0:T(8,128)(2,1)}) custom-call(bf16[1792,128]{1,0:T(8,128)(2,1)} %get-tuple-element.29.refs_0_, bf16[1792,128]{1,0:T(8,128)(2,1)} %get-tuple-element.30.refs_1_), custom_call_target="tpu_custom_call" | custom-call | tf_op jit(solution)/shard_map/gather_bc/pallas_call | solution.py:554
  126.2 173.9 %mttkrp_a.1 = f32[37888,128]{1,0:T(8,128)} custom-call(s32[1]{0:T(128)} %bitcast.nblk_ref, s32[512]{0:T(512)} %reshape.141.flag_ref, s32[65536]{0:T(1024)} %get-tuple-element.75.out_h, s32[65536]{0:T(1024)} %copy-done.1, s32[65536]{0:T(1024)} %copy-done.3, f32[512,128]{1,0:T(8,128)} %bitcast.60, s32[512,128]{1,0:T(8,128)} %get-tuple-element.81.code_ref, ...), custom_call_target="tpu_custom_call" | custom-call | flops 2000000000 | bytes 50000000 | tf_op jit(solution)/shard_map/mttkrp_a/pallas_call | solution.py:250
  300.2 220.6 %fold_a.1.m_ref = f32[4736,128]{1,0:T(8,128)} custom-call(f32[4,2,4736,128]{3,2,1,0:T(8,128)} %bitcast.57), custom_call_target="tpu_custom_call" | custom-call | tf_op jit(solution)/shard_map/fold_a/pallas_call | solution.py:759
  520.8 23.9 %solve_a.1 = (f32[64,9408]{1,0:T(8,128)}, f32[64,64]{1,0:T(8,128)}) custom-call(f32[4736,128]{1,0:T(8,128)} %fold_a.1.m_ref, f32[64,9408]{1,0:T(8,128)} %bitcast.67, f32[64,64]{1,0:T(8,128)} %get-tuple-element.34.inv_ref, f32[8,128]{1,0:T(8,128)} %get-tuple-element.35.mu_ref), custom_call_target="tpu_custom_call" | custom-call | tf_op jit(solution)/shard_map/solve_a/pallas_call | solution.py:398
  544.7 13.0 sum_a.1.gram_ref
  557.7 7.3 scale_a.1
  565.0 7.6 invert_b.1
  572.6 135.8 %gather_a.1.tab1_h = bf16[37888,128]{1,0:T(8,128)(2,1)} custom-call(bf16[4736,128]{1,0:T(8,128)(2,1)} %get-tuple-element.39.refs_0_), custom_call_target="tpu_custom_call" | custom-call | tf_op jit(solution)/shard_map/gather_a/pallas_call | solution.py:554
  708.4 172.8 %mttkrp_b.1 = f32[28672,128]{1,0:T(8,128)} custom-call(s32[1]{0:T(128)} %bitcast.nblk_ref, s32[512]{0:T(512)} %reshape.145.flag_ref, s32[65536]{0:T(1024)} %get-tuple-element.73.out_h, s32[65536]{0:T(1024)} %copy-done.2, s32[65536]{0:T(1024)} %copy-done.3, f32[512,128]{1,0:T(8,128)} %bitcast.61, s32[512,128]{1,0:T(8,128)} %get-tuple-element.80.code_ref, ...), custom_call_target="tpu_custom_call" | custom-call | flops 2000000000 | bytes 50000000 | tf_op jit(solution)/shard_map/mttkrp_b/pallas_call | solution.py:250
  881.2 124.2 %fold_b.1.m_ref = f32[1792,128]{1,0:T(8,128)} custom-call(f32[4,2,2,1792,128]{4,3,2,1,0:T(8,128)} %bitcast.58), custom_call_target="tpu_custom_call" | custom-call | tf_op jit(solution)/shard_map/fold_b/pallas_call | solution.py:759
  1005.4 9.7 solve_b.1
  1015.1 12.7 sum_b.1.gram_ref
  1027.8 3.6 scale_b.1
  1031.4 7.6 invert_c.1
  1039.0 55.4 %gather_b.1.tab2_h = bf16[28672,128]{1,0:T(8,128)(2,1)} custom-call(bf16[1792,128]{1,0:T(8,128)(2,1)} %get-tuple-element.46.refs_0_), custom_call_target="tpu_custom_call" | custom-call | tf_op jit(solution)/shard_map/gather_b/pallas_call | solution.py:554
  1094.4 175.2 %mttkrp_c.1 = f32[14336,128]{1,0:T(8,128)} custom-call(s32[1]{0:T(128)} %bitcast.nblk_ref, s32[512]{0:T(512)} %reshape.148.flag_ref, s32[65536]{0:T(1024)} %get-tuple-element.61.out_h, s32[65536]{0:T(1024)} %copy-done.2, s32[65536]{0:T(1024)} %copy-done.1, f32[512,128]{1,0:T(8,128)} %bitcast.62, s32[512,128]{1,0:T(8,128)} %get-tuple-element.79.code_ref, ...), custom_call_target="tpu_custom_call" | custom-call | flops 2000000000 | bytes 50000000 | tf_op jit(solution)/shard_map/mttkrp_c/pallas_call | solution.py:250
  1269.6 59.6 %fold_c.1.m_ref = f32[1792,128]{1,0:T(8,128)} custom-call(f32[2,2,2,1792,128]{4,3,2,1,0:T(8,128)} %bitcast.59), custom_call_target="tpu_custom_call" | custom-call | tf_op jit(solution)/shard_map/fold_c/pallas_call | solution.py:759
  1329.2 9.8 solve_c.1
  1339.0 13.6 %sum_c.1.gram_ref = f32[64,64]{1,0:T(8,128)} custom-call(f32[64,64]{1,0:T(8,128)} %get-tuple-element.51.x_ref), custom_call_target="tpu_custom_call" | custom-call | tf_op jit(solution)/shard_map/sum_c/pallas_call | solution.py:601
  1352.6 2.3 scale_c.1
  (32 shorter events, 1.8 us)
Async XLA Ops:
  0.6 6.5 copy-start.4
  0.6 6.5 copy-start.5
  0.7 7.1 copy-start.6
  3.8 5.8 copy-start
  10.6 115.7 %copy-start.3 = (s32[65536]{0:T(1024)}, s32[65536]{0:T(1024)S(1)}, u32[]{:S(2)}) copy-start(s32[65536]{0:T(1024)S(1)} %get-tuple-element.55.two_h) | copy-start | bytes 786436
  49.8 0.7 copy-start.1
  49.8 2.3 copy-start.2
